TPU v7x, 32 devices: a whole 2x2x4 slice. The times are simulated.
32 devices in a mesh: row: 4 (over x, core), col: 4 (over z), depth: 2 (over y).
Axes of the slice: x: 2, y: 2, z: 4, core: 2. Of those that a mesh axis runs over, the one named last changes fastest.
Arguments:
- trailing: float32 [3008, 48128], P('depth', ('row', 'col')), may hold values from -6 to 6
- panel_block: float32 [48128, 1024], P(('row', 'col', 'depth')), may hold values from -6 to 6
- factor_panel: float32 [48128, 1024], P(('row', 'col', 'depth')), may hold values from -0.1875 to 0.1875
- corner_block: float32 [1024, 1024], P(('row', 'col', 'depth')), may hold values from -6 to 6, as said below
- corner_inverse: float32 [1024, 1024], P(('row', 'col', 'depth')), may hold values from -1 to 2, as said below
Outputs:
- trailing_out: float32 [3008, 48128], P('depth', ('row', 'col'))
- panel_out: float32 [48128, 1024], P(('row', 'col', 'depth'))
- corner_out: float32 [1024, 1024], P(('row', 'col', 'depth'))
Inputs may be any that keep to these rules, and one draw needn't show every extreme that they name: `corner_block`: symmetric. `corner_inverse`: lower triangular, diagonal between 1 and 2.
All inputs are finite; a program needn't handle non-finite values.
Results may differ from a plain program's by a relative error of at most 0.00012.
Values sent between devices are 32-bit elements; how exact they have to be, the bound alone decides.
A program may use at most 192 MiB of HBM per device.

v0:
```python
import jax
import jax.numpy as jnp
from jax import lax
from jax.sharding import PartitionSpec as P

EVERY = ("row", "col", "depth")
PIECES = 1


def matmul(left, right):
    return jnp.dot(left, right, precision=lax.Precision.HIGH, preferred_element_type=jnp.float32)


def contract(left, right):
    return lax.dot_general(
        left,
        right,
        (((1,), (1,)), ((), ())),
        precision=lax.Precision.HIGH,
        preferred_element_type=jnp.float32,
    )


def after(value, earlier):
    return lax.optimization_barrier((value, earlier))[0]


def gather_corner(corner_block, corner_inverse):
    rows, width = corner_inverse.shape
    first = lax.axis_index(EVERY) * rows
    row = first + lax.broadcasted_iota(jnp.int32, (rows, width), 0)
    col = lax.broadcasted_iota(jnp.int32, (rows, width), 1)
    both = jnp.where(col > row, corner_block, corner_inverse)
    diagonal = jnp.sum(jnp.where(col == row, corner_block, 0.0), axis=1, keepdims=True)
    packed = jnp.concatenate([both, jnp.broadcast_to(diagonal, (rows, 128))], axis=1)
    return lax.all_gather(packed, EVERY, axis=0, tiled=True)


def unpack_corner(packed, width):
    row = lax.broadcasted_iota(jnp.int32, (width, width), 0)
    col = lax.broadcasted_iota(jnp.int32, (width, width), 1)
    both = packed[:, :width]
    inverse = jnp.where(col <= row, both, 0.0)
    upper = jnp.where(col > row, both, jnp.where(col == row, 0.5 * packed[:, width:width + 1], 0.0))
    return inverse, upper


def transform(panel, factor, inverse, corner):
    coupling = matmul(factor, corner)
    half = contract(panel, inverse) - 0.5 * coupling
    return half - 0.5 * coupling


def exchange(value, layers):
    blocks = [value]
    for shift in range(1, layers):
        pairs = [(source, (source + shift) % layers) for source in range(layers)]
        blocks.append(lax.ppermute(value, "depth", pairs))
    return blocks


def arrange(blocks, layers):
    if layers == 1:
        return blocks[0]
    me = lax.axis_index("depth")
    rows, width = blocks[0].shape
    whole = jnp.zeros((layers * rows, width), blocks[0].dtype)
    for shift, block in enumerate(blocks):
        place = lax.rem(me - shift + layers, layers)
        whole = lax.dynamic_update_slice(whole, block, (place * rows, 0))
    return whole


def make_body(layers):
    def body(trailing, panel_block, factor_panel, corner_block, corner_inverse):
        rows, width = panel_block.shape
        factor_blocks = exchange(factor_panel, layers)
        panel_blocks = exchange(panel_block, layers)
        packed = gather_corner(corner_block, corner_inverse)

        count = PIECES if rows % PIECES == 0 else 1
        size = rows // count
        source = lax.axis_index(("row", "col")) == 0
        slabs = []
        for piece in range(count):
            part = slice(piece * size, (piece + 1) * size)
            pair = (panel_block[part], factor_panel[part])
            if piece:
                pair = after(pair, slabs[-1])
            kept = jnp.where(source, jnp.concatenate(pair, axis=0), 0.0)
            slabs.append(lax.psum(kept, ("row", "col")))

        inverse, upper = unpack_corner(packed, width)
        triangle = matmul(inverse, contract(upper, inverse))
        corner = triangle + triangle.T
        corner_rows = corner_inverse.shape[0]
        corner_out = lax.dynamic_slice(
            corner, (lax.axis_index(EVERY) * corner_rows, 0), (corner_rows, width)
        )
        panel_out = transform(panel_block, factor_panel, inverse, corner)

        factor_cols = arrange(factor_blocks, layers)
        panel_cols = arrange(panel_blocks, layers)
        outs = []
        for piece in range(count):
            panel_piece, factor_piece = slabs[piece][:size], slabs[piece][size:]
            left = transform(panel_piece, factor_piece, inverse, corner)
            right = matmul(factor_piece, inverse)
            part = trailing[piece * size:(piece + 1) * size]
            outs.append((part - contract(left, factor_cols)) - contract(right, panel_cols))
        trailing_out = jnp.concatenate(outs, axis=0)
        return (trailing_out, panel_out, corner_out)

    return body


def solution(mesh):
    in_specs = (
        P("depth", ("row", "col")),
        P(EVERY, None),
        P(EVERY, None),
        P(EVERY, None),
        P(EVERY, None),
    )
    out_specs = (
        P("depth", ("row", "col")),
        P(EVERY, None),
        P(EVERY, None),
    )
    body = make_body(mesh.shape["depth"])
    return jax.shard_map(body, mesh=mesh, in_specs=in_specs, out_specs=out_specs, check_vma=False)
```

profile of v0, /device:TPU:0, one launch (start us, length us, event | category | flops | bytes accessed | tf_op | source)
XLA Modules:
  0.0 476.8 jit_solution(9041454763933964617)
XLA Ops:
  8.1 1.2 fusion.32
  10.1 3.1 collective-permute-start
  13.2 12.1 %maximum_select_fusion = f32[3008,1024]{1,0:T(8,128)} fusion(f32[1504,1024]{1,0:T(8,128)} %param.7, f32[1504,1024]{1,0:T(8,128)} %param.6, pred[]{:T(512)S(6)} %eq.9), kind=kLoop, calls=%fused_computation.1 | loop fusion | flops 6160384 | bytes 24641536 | tf_op jit(solution)/shard_map/jit(_where)/select_n | solution.py:90
  25.4 6.0 %broadcast_in_dim.30.clone = f32[3008,1024]{1,0:T(8,128)} broadcast(f32[]{:T(128)} %constant.11.clone.1), dimensions={} | broadcast | bytes 12320772 | tf_op jit(solution)/shard_map/jit(_where)/broadcast_in_dim | solution.py:90
  31.4 7.3 %constant_dynamic-update-slice_fusion.3 = f32[3008,1024]{1,0:T(8,128)} fusion(f32[3008,1024]{1,0:T(8,128)} %broadcast_in_dim.30.clone, f32[1504,1024]{1,0:T(8,128)} %param.7, s32[]{:T(128)S(6)} %select_n.46), kind=kLoop, calls=%fused_computation.45 | loop fusion | bytes 12320772 | tf_op jit(solution)/shard_map/dynamic_update_slice | solution.py:70
  38.7 6.0 %broadcast_in_dim.30.clone.1 = f32[3008,1024]{1,0:T(8,128)} broadcast(f32[]{:T(128)} %constant.11.clone.1), dimensions={} | broadcast | bytes 12320772 | tf_op jit(solution)/shard_map/jit(_where)/broadcast_in_dim | solution.py:90
  44.7 3.2 constant_dynamic-update-slice_fusion.1
  47.9 110.7 %collective-permute-done = f32[1504,1024]{1,0:T(8,128)} collective-permute-done((f32[1504,1024]{1,0:T(8,128)}, f32[1504,1024]{1,0:T(8,128)}, u32[]{:S(2)}, u32[]{:S(2)}) %collective-permute-start) | collective-permute-done | bytes 6160416 | tf_op jit(solution)/shard_map/ppermute | solution.py:58
  158.6 6.4 %constant_dynamic-update-slice_fusion.2 = f32[3008,1024]{1,0:T(8,128)} fusion(f32[3008,1024]{1,0:T(8,128)} %constant_dynamic-update-slice_fusion.3, f32[1504,1024]{1,0:T(8,128)} %collective-permute-done, s32[]{:T(128)S(6)} %select_n.47), kind=kLoop, calls=%fused_computation.44 | loop fusion | bytes 12320772 | tf_op jit(solution)/shard_map/dynamic_update_slice | solution.py:70
  165.0 124.7 %collective-permute-done.1 = f32[1504,1024]{1,0:T(8,128)} collective-permute-done((f32[1504,1024]{1,0:T(8,128)}, f32[1504,1024]{1,0:T(8,128)}, u32[]{:S(2)}, u32[]{:S(2)}) %collective-permute-start.1) | collective-permute-done | bytes 6160416 | tf_op jit(solution)/shard_map/ppermute | solution.py:58
  289.8 6.4 %constant_dynamic-update-slice_fusion = f32[3008,1024]{1,0:T(8,128)} fusion(f32[3008,1024]{1,0:T(8,128)} %constant_dynamic-update-slice_fusion.1, f32[1504,1024]{1,0:T(8,128)} %collective-permute-done.1, s32[]{:T(128)S(6)} %select_n.47), kind=kLoop, calls=%fused_computation.42 | loop fusion | bytes 12320772 | tf_op jit(solution)/shard_map/dynamic_update_slice | solution.py:70
  296.2 1.4 fusion.31
  297.6 10.8 %fusion.8 = f32[1024,1024]{1,0:T(8,128)S(1)} fusion(f32[1024,1152]{1,0:T(8,128)} %all-gather.2.cloned.1.call-done, f32[1024]{0:T(1024)S(1)} %fusion.31), kind=kOutput, calls=%fused_computation.13 | convolution fusion | flops 6448742400 | bytes 12587008 | tf_op jit(solution)/shard_map/dot_general | solution.py:15
  308.4 8.2 %fusion.15 = f32[1024,1024]{1,0:T(8,128)} fusion(f32[1024,1024]{1,0:T(8,128)S(1)} %fusion.8, f32[1024,1152]{1,0:T(8,128)S(1)} %bitcast.21), kind=kOutput, calls=%fused_computation.21 | convolution fusion | flops 6444548096 | bytes 12582912 | tf_op jit(solution)/shard_map/dot_general | solution.py:11
  316.7 5.5 %copy.9 = f32[1024,1024]{0,1:T(8,128)} copy(f32[1024,1024]{1,0:T(8,128)} %fusion.15) | data formatting | bytes 8388608 | tf_op jit(solution)/shard_map/dot_general | solution.py:11
  322.1 5.0 %bitcast_add_fusion = f32[1024,1024]{1,0:T(8,128)S(1)} fusion(f32[1024,1024]{1,0:T(8,128)} %fusion.15, f32[1024,1024]{0,1:T(8,128)} %copy.9), kind=kLoop, calls=%fused_computation.12 | loop fusion | flops 1048576 | bytes 12582912 | tf_op jit(solution)/shard_map/add | solution.py:95
  327.1 0.7 constant_dynamic-slice_fusion
  327.9 15.0 %fusion.12 = f32[1024,1504]{0,1:T(8,128)S(1)} fusion(f32[1504,1024]{1,0:T(8,128)S(1)} %bitcast.17, f32[1024,1152]{1,0:T(8,128)} %all-gather.2.cloned.1.call-done), kind=kOutput, calls=%fused_computation.20 | convolution fusion | flops 9464446976 | bytes 16515072 | tf_op jit(solution)/shard_map/dot_general | solution.py:15
  342.9 11.7 %subtract_subtract_fusion.1 = f32[1504,1024]{1,0:T(8,128)} fusion(f32[1024,1504]{0,1:T(8,128)S(1)} %fusion.12, f32[1024,1024]{1,0:T(8,128)S(1)} %bitcast_add_fusion, f32[1504,1024]{1,0:T(8,128)S(1)} %bitcast.19), kind=kOutput, calls=%fused_computation.2 | convolution fusion | flops 9466970112 | bytes 22675456 | tf_op jit(solution)/shard_map/dot_general | solution.py:11
  354.6 13.5 %fusion.6 = f32[1504,1024]{1,0:T(8,128)S(1)} fusion(f32[1024,1024]{1,0:T(8,128)} %copy-done, f32[3008,1024]{1,0:T(8,128)} %all-reduce.2.cloned.1.call-done), kind=kOutput, calls=%fused_computation.10 | convolution fusion | flops 9462349824 | bytes 16515072 | tf_op jit(solution)/shard_map/dot_general | solution.py:11
  368.1 13.6 %fusion.1 = f32[1504,1024]{1,0:T(8,128)} fusion(f32[3008,1024]{1,0:T(8,128)S(1)} %copy-done.1, f32[1024,1152]{1,0:T(8,128)} %all-gather.2.cloned.1.call-done), kind=kOutput, calls=%fused_computation.5 | convolution fusion | flops 9464446976 | bytes 16515072 | tf_op jit(solution)/shard_map/dot_general | solution.py:15
  381.7 37.4 %fusion = f32[1504,3008]{1,0:T(8,128)} fusion(f32[3008,1024]{1,0:T(8,128)} %constant_dynamic-update-slice_fusion.2, f32[1504,1024]{1,0:T(8,128)} %fusion.1, f32[1504,1024]{1,0:T(8,128)S(1)} %fusion.6), kind=kOutput, calls=%fused_computation.4 | convolution fusion | flops 27800272896 | bytes 42737664 | tf_op jit(solution)/shard_map/dot_general | solution.py:15
  419.1 11.9 %fusion.4 = f32[1504,1024]{1,0:T(8,128)S(1)} fusion(f32[3008,1024]{1,0:T(8,128)} %all-reduce.2.cloned.1.call-done, f32[1024,1152]{1,0:T(8,128)S(1)} %bitcast.23), kind=kOutput, calls=%fused_computation.8 | convolution fusion | flops 9464446976 | bytes 16515072 | tf_op jit(solution)/shard_map/dot_general | solution.py:11
  431.0 37.8 %subtract_subtract_fusion = f32[1504,3008]{1,0:T(8,128)} fusion(f32[1504,3008]{1,0:T(8,128)} %param.5, f32[1504,3008]{1,0:T(8,128)} %fusion, f32[1504,1024]{1,0:T(8,128)S(1)} %fusion.4, f32[3008,1024]{1,0:T(8,128)} %constant_dynamic-update-slice_fusion), kind=kOutput, calls=%fused_computation | convolution fusion | flops 27804700672 | bytes 72769536 | tf_op jit(solution)/shard_map/dot_general | solution.py:15
  (39 shorter events, 1.0 us)
Async XLA Ops:
  8.0 288.2 %all-gather.2.cloned.1.call-start = ((), (), s32[]{:S(2)}) async-start(), calls=%async_computation.1 | async-start | bytes 4866048 | tf_op jit(solution)/shard_map/all_gather | solution.py:36
  10.0 344.6 %all-reduce.2.cloned.1.call-start = ((), (), s32[]{:S(2)}) async-start(), calls=%async_computation | async-start | bytes 24641536 | tf_op jit(solution)/shard_map/psum | solution.py:91
  10.1 148.5 %collective-permute-start = (f32[1504,1024]{1,0:T(8,128)}, f32[1504,1024]{1,0:T(8,128)}, u32[]{:S(2)}, u32[]{:S(2)}) collective-permute-start(f32[1504,1024]{1,0:T(8,128)} %param.7), channel_id=1, source_target_pairs={{0,1},{1,0},{2,3},{3,2},{4,5},{5,4},{6,7},{7,6},{8,9},{9,8},{10,11... | collective-permute-start | bytes 18481160 | tf_op jit(solution)/shard_map/ppermute | solution.py:58
  13.1 276.6 %collective-permute-start.1 = (f32[1504,1024]{1,0:T(8,128)}, f32[1504,1024]{1,0:T(8,128)}, u32[]{:S(2)}, u32[]{:S(2)}) collective-permute-start(f32[1504,1024]{1,0:T(8,128)} %param.6), channel_id=1, source_target_pairs={{0,1},{1,0},{2,3},{3,2},{4,5},{5,4},{6,7},{7,6},{8,9},{9,8},{10,11... | collective-permute-start | bytes 18481160 | tf_op jit(solution)/shard_map/ppermute | solution.py:58
  31.4 13.4 %slice-start = ((s8[6160384]{0:T(1024)(128)(4,1)}), s8[4194304]{0:T(1024)(128)(4,1)S(1)}, s32[]{:S(2)}) async-start(s8[6160384]{0:T(1024)(128)(4,1)} %bitcast.14), calls=%async_computation.2 | async-start | bytes 8388608
  38.7 6.0 %slice-start.1 = ((s8[6160384]{0:T(1024)(128)(4,1)}), s8[1966080]{0:T(1024)(128)(4,1)S(1)}, s32[]{:S(2)}) async-start(s8[6160384]{0:T(1024)(128)(4,1)} %bitcast.14), calls=%async_computation.3 | async-start | bytes 3932160
  296.2 12.2 %slice-start.6 = ((s8[4718592]{0:T(1024)(128)(4,1)}), s8[4194304]{0:T(1024)(128)(4,1)S(1)}, s32[]{:S(2)}) async-start(s8[4718592]{0:T(1024)(128)(4,1)} %bitcast.20), calls=%async_computation.8 | async-start | bytes 8388608
  297.6 10.8 %slice-start.7 = ((s8[4718592]{0:T(1024)(128)(4,1)}), s8[524288]{0:T(1024)(128)(4,1)S(1)}, s32[]{:S(2)}) async-start(s8[4718592]{0:T(1024)(128)(4,1)} %bitcast.20), calls=%async_computation.9 | async-start | bytes 1048576
  316.7 11.2 %slice-start.2 = ((s8[6160384]{0:T(1024)(128)(4,1)}), s8[1966080]{0:T(1024)(128)(4,1)S(1)}, s32[]{:S(2)}) async-start(s8[6160384]{0:T(1024)(128)(4,1)} %bitcast.16), calls=%async_computation.4 | async-start | bytes 3932160
  322.1 5.7 %slice-start.3 = ((s8[6160384]{0:T(1024)(128)(4,1)}), s8[4194304]{0:T(1024)(128)(4,1)S(1)}, s32[]{:S(2)}) async-start(s8[6160384]{0:T(1024)(128)(4,1)} %bitcast.16), calls=%async_computation.5 | async-start | bytes 8388608
  322.1 20.7 %slice-start.4 = ((s8[6160384]{0:T(1024)(128)(4,1)}), s8[4194304]{0:T(1024)(128)(4,1)S(1)}, s32[]{:S(2)}) async-start(s8[6160384]{0:T(1024)(128)(4,1)} %bitcast.18), calls=%async_computation.6 | async-start | bytes 8388608
  327.1 15.7 %copy-start = (f32[1024,1024]{1,0:T(8,128)}, f32[1024,1024]{1,0:T(8,128)S(1)}, u32[]{:S(2)}) copy-start(f32[1024,1024]{1,0:T(8,128)S(1)} %bitcast_add_fusion) | copy-start | bytes 12582916
  327.9 15.0 %slice-start.5 = ((s8[6160384]{0:T(1024)(128)(4,1)}), s8[1966080]{0:T(1024)(128)(4,1)S(1)}, s32[]{:S(2)}) async-start(s8[6160384]{0:T(1024)(128)(4,1)} %bitcast.18), calls=%async_computation.7 | async-start | bytes 3932160
  354.6 13.5 %copy-start.1 = (f32[3008,1024]{1,0:T(8,128)S(1)}, f32[3008,1024]{1,0:T(8,128)}, u32[]{:S(2)}) copy-start(f32[3008,1024]{1,0:T(8,128)} %all-reduce.2.cloned.1.call-done) | copy-start | bytes 36962308
  368.1 51.0 %slice-start.8 = ((s8[4718592]{0:T(1024)(128)(4,1)}), s8[4194304]{0:T(1024)(128)(4,1)S(1)}, s32[]{:S(2)}) async-start(s8[4718592]{0:T(1024)(128)(4,1)} %bitcast.22), calls=%async_computation.10 | async-start | bytes 8388608
  381.7 37.4 %slice-start.9 = ((s8[4718592]{0:T(1024)(128)(4,1)}), s8[524288]{0:T(1024)(128)(4,1)S(1)}, s32[]{:S(2)}) async-start(s8[4718592]{0:T(1024)(128)(4,1)} %bitcast.22), calls=%async_computation.11 | async-start | bytes 1048576
Sparse Core Ops, SparseCore 0:
  12.3 97.3 all-gather.1
Sparse Core Ops, SparseCore 1:
  25.5 249.3 all-reduce.1
where the time goes:
time: 482 us; the launch traced here: 477 us
  waiting for transfers between devices  235 us (49%)
  matrix products  160 us (33%)
  local copies, waits for them, and re-layouts  41.7 us (9%)
  other arithmetic  20.4 us (4%)
  between operations  16.1 us (3%)
    ppermute x2, waiting for transfers between devices, exchange(): blocks.append(lax.ppermute(value, 'depth', pairs))  235 us
    dot_general x5, matrix products, contract(): lax.dot_general(left, right, (((1,), (1,)), ((), ())), precision=lax.Prec...  115 us
    dot_general x4, matrix products, matmul(): jnp.dot(left, right, precision=lax.Precision.HIGH, preferred_element_type...  45.3 us
    dynamic_update_slice x4, local copies, waits for them, and re-layouts, arrange(): whole = lax.dynamic_update_slice(whole, block, (place * rows, 0))  23.4 us
    select_n x1, other arithmetic, body(): kept = jnp.where(source, jnp.concatenate(pair, axis=0), 0.0)  12.1 us
    broadcast_in_dim x2, local copies, waits for them, and re-layouts, body(): kept = jnp.where(source, jnp.concatenate(pair, axis=0), 0.0)  12 us
  transfers between devices with their start and end apart: 4, of which 2 were waited for; matrix products, arithmetic and copies ran while one was open for 22% of the time, Pallas kernels for 0%

commit v1 on v0

v1 whole, which is shorter than its diff:
```python
import functools

import jax
import jax.numpy as jnp
from jax import lax
from jax.experimental import pallas as pl
from jax.experimental.pallas import tpu as pltpu
from jax.sharding import PartitionSpec as P


EVERY = ("row", "col", "depth")
MESH = pl.DeviceIdType.MESH
TILE = 256
LIMIT = 60 * 1024 * 1024
ANY = pl.BlockSpec(memory_space=pl.ANY)


def matmul(left, right):
    return jnp.dot(left, right, precision=lax.Precision.HIGH, preferred_element_type=jnp.float32)


def contract(left, right):
    return lax.dot_general(
        left,
        right,
        (((1,), (1,)), ((), ())),
        precision=lax.Precision.HIGH,
        preferred_element_type=jnp.float32,
    )


def pack_corner(corner_block, corner_inverse):
    rows, width = corner_inverse.shape
    first = lax.axis_index(EVERY) * rows
    row = first + lax.broadcasted_iota(jnp.int32, (rows, width), 0)
    col = lax.broadcasted_iota(jnp.int32, (rows, width), 1)
    both = jnp.where(col > row, corner_block, corner_inverse)
    diagonal = jnp.sum(jnp.where(col == row, corner_block, 0.0), axis=1, keepdims=True)
    return jnp.concatenate([both, jnp.broadcast_to(diagonal, (rows, 128))], axis=1)


def unpack_corner(packed, width):
    row = lax.broadcasted_iota(jnp.int32, (width, width), 0)
    col = lax.broadcasted_iota(jnp.int32, (width, width), 1)
    both = packed[:, :width]
    inverse = jnp.where(col <= row, both, 0.0)
    upper = jnp.where(col > row, both, jnp.where(col == row, 0.5 * packed[:, width:width + 1], 0.0))
    return inverse, upper


def transform(panel, factor, inverse, corner):
    coupling = matmul(factor, corner)
    half = contract(panel, inverse) - 0.5 * coupling
    return half - 0.5 * coupling


def exchange(value, layers):
    blocks = [value]
    for shift in range(1, layers):
        pairs = [(source, (source + shift) % layers) for source in range(layers)]
        blocks.append(lax.ppermute(value, "depth", pairs))
    return blocks


def arrange(blocks, layers):
    if layers == 1:
        return blocks[0]
    me = lax.axis_index("depth")
    rows, width = blocks[0].shape
    whole = jnp.zeros((layers * rows, width), blocks[0].dtype)
    for shift, block in enumerate(blocks):
        place = lax.rem(me - shift + layers, layers)
        whole = lax.dynamic_update_slice(whole, block, (place * rows, 0))
    return whole


def make_general(layers):
    def body(trailing, panel_block, factor_panel, corner_block, corner_inverse):
        rows, width = panel_block.shape
        factor_blocks = exchange(factor_panel, layers)
        panel_blocks = exchange(panel_block, layers)
        packed = lax.all_gather(pack_corner(corner_block, corner_inverse), EVERY, axis=0, tiled=True)
        source = lax.axis_index(("row", "col")) == 0
        kept = jnp.where(source, jnp.concatenate((panel_block, factor_panel), axis=0), 0.0)
        slab = lax.psum(kept, ("row", "col"))
        inverse, upper = unpack_corner(packed, width)
        triangle = matmul(inverse, contract(upper, inverse))
        corner = triangle + triangle.T
        corner_rows = corner_inverse.shape[0]
        corner_out = lax.dynamic_slice(
            corner, (lax.axis_index(EVERY) * corner_rows, 0), (corner_rows, width)
        )
        panel_out = transform(panel_block, factor_panel, inverse, corner)
        factor_cols = arrange(factor_blocks, layers)
        panel_cols = arrange(panel_blocks, layers)
        left = transform(slab[:rows], slab[rows:], inverse, corner)
        right = matmul(slab[rows:], inverse)
        trailing_out = (trailing - contract(left, factor_cols)) - contract(right, panel_cols)
        return (trailing_out, panel_out, corner_out)

    return body


def after(value, earlier):
    return lax.optimization_barrier((value, earlier))[0]


def spread_kernel(ncol, piece, packed, panel, factor, corner, ps, fs,
                  yl, zr, zl, xr, cr, sz, sx, sc, rm, rp, su, sd, sq):
    r, c, d = lax.axis_index("row"), lax.axis_index("col"), lax.axis_index("depth")
    x, core = r // 2, r % 2
    across, mate = (1 - x) * 2 + core, x * 2 + (1 - core)
    block = packed.shape[0]
    count = ps.shape[0] // piece
    source = (r == 0) & (c == 0)

    def at(ref, first, size):
        return ref.at[pl.ds(pl.multiple_of(first, 8), size)]

    def remote(src, dst, send, recv, row, col, depth):
        return pltpu.make_async_remote_copy(
            src_ref=src, dst_ref=dst, send_sem=send, recv_sem=recv,
            device_id=(row, col, depth), device_id_type=MESH)

    keep = pltpu.make_async_copy(packed, at(corner, (r * ncol + c) * block, block), yl)
    keep.start()

    def each(body):
        def step(k, carry):
            body(k, pl.ds(pl.multiple_of(k * piece, 8), piece))
            return carry

        lax.fori_loop(0, count, step, 0)

    keep.wait()

    def rows_of(row, col):
        return at(corner, (row * ncol + col) * block, block)

    def forward_line(col, right, left):
        b = rows_of(r, col)

        if right:
            @pl.when(c < ncol - 1)
            def _():
                remote(b, b, sz.at[0, col], zr.at[col], r, c + 1, d).start()
        if left:
            @pl.when(c > 0)
            def _():
                remote(b, b, sz.at[1, col], zl.at[col], r, c - 1, d).start()
        remote(b, b, sx.at[col], xr.at[col], across, c, d).start()
        remote(b, b, sc.at[0, col], cr.at[0, col], mate, c, d).start()

    forward_line(c, True, True)

    @pl.when(source)
    def _():
        def body(k, s):
            remote(factor.at[s], fs.at[s], su, rm.at[k], 0, 1, d).start()
            remote(panel.at[s], ps.at[s], sd, rm.at[k], 3, 0, d).start()
            remote(factor.at[s], fs.at[s], sq.at[0], rp, 1, 0, d).start()
            remote(panel.at[s], ps.at[s], sq.at[1], rm.at[k], 1, 0, d).start()

        each(body)

    for s in range(1, ncol):
        @pl.when(c - s >= 0)
        def _():
            b = rows_of(r, c - s)
            remote(b, b, sz.at[0, c - s], zr.at[c - s], r, c, d).wait_recv()
            forward_line(c - s, True, False)

        @pl.when(c + s < ncol)
        def _():
            b = rows_of(r, c + s)
            remote(b, b, sz.at[1, c + s], zl.at[c + s], r, c, d).wait_recv()
            forward_line(c + s, False, True)

    def across_block(col):
        b = rows_of(across, col)
        remote(b, b, sx.at[col], xr.at[col], across, c, d).wait_recv()
        remote(b, b, sc.at[1, col], cr.at[1, col], mate, c, d).start()

    across_block(c)
    for s in range(1, ncol):
        @pl.when(c - s >= 0)
        def _():
            across_block(c - s)

        @pl.when(c + s < ncol)
        def _():
            across_block(c + s)

    trunk = x == core

    def stream(ref, other, own):
        up = trunk & (c < ncol - 1) & jnp.logical_not(source)
        side = trunk & (c > 0)
        down = (own == 0) & (x == 1) & (c == 1)
        local = (x > 0) | (c > 0)

        @pl.when(jnp.logical_not(source))
        def _():
            def body(k, s):
                v = ref.at[s]
                remote(v, v, su, rm.at[k], r, c, d).wait_recv()

                @pl.when(up)
                def _():
                    remote(v, v, su, rm.at[k], r, c + 1, d).start()

                @pl.when(side)
                def _():
                    remote(v, v, sd, rm.at[k], across, c, d).start()

                @pl.when(down)
                def _():
                    remote(v, v, sd, rm.at[k], r, 0, d).start()

                @pl.when(local)
                def _():
                    remote(v, v, sq.at[0], rp, mate, c, d).start()

            each(body)
            remote(other, other, su, rp, r, c, d).wait_recv()

            @pl.when(up)
            def _():
                remote(ref, ref, su, rp, r, c, d).wait_send()

            @pl.when(side | down)
            def _():
                remote(ref, ref, sd, rp, r, c, d).wait_send()

            @pl.when(local)
            def _():
                remote(ref, ref, sq.at[0], rp, r, c, d).wait_send()

    @pl.when(core == 0)
    def _():
        stream(fs, ps, 0)

    @pl.when(core == 1)
    def _():
        stream(ps, fs, 1)

    @pl.when(source)
    def _():
        for sem in (su, sd, sq.at[0], sq.at[1]):
            remote(ps, ps, sem, rp, r, c, d).wait_send()

    for col in range(ncol):
        for half in range(2):
            b = rows_of(0, col)
            remote(b, b, sc.at[half, col], cr.at[half, col], mate, c, d).wait()
        remote(b, b, sx.at[col], rp, r, c, d).wait_send()

        @pl.when((c < ncol - 1) & (col <= c))
        def _():
            b = rows_of(0, col)
            remote(b, b, sz.at[0, col], rp, r, c, d).wait_send()

        @pl.when((c > 0) & (col >= c))
        def _():
            b = rows_of(0, col)
            remote(b, b, sz.at[1, col], rp, r, c, d).wait_send()


def spread(packed, panel, factor, ncol, devices):
    rows = panel.shape[0]
    piece = 32
    count = rows // piece
    dma = pltpu.SemaphoreType.DMA
    return pl.pallas_call(
        functools.partial(spread_kernel, ncol, piece),
        out_shape=(
            jax.ShapeDtypeStruct((packed.shape[0] * devices // 2, packed.shape[1]), jnp.float32),
            jax.ShapeDtypeStruct(panel.shape, jnp.float32),
            jax.ShapeDtypeStruct(panel.shape, jnp.float32),
        ),
        in_specs=[ANY] * 3,
        out_specs=(ANY,) * 3,
        scratch_shapes=[
            dma, dma((ncol,)), dma((ncol,)), dma((ncol,)), dma((2, ncol)),
            dma((2, ncol)), dma((ncol,)), dma((2, ncol)),
            dma((count,)), dma, dma, dma, dma((2,)),
        ],
        compiler_params=pltpu.CompilerParams(has_side_effects=True, vmem_limit_bytes=8 * 1024 * 1024),
        cost_estimate=pl.CostEstimate(flops=100_000_000, bytes_accessed=40_000_000, transcendentals=0),
        name="spread",
    )(packed, panel, factor)


def halves(value):
    high = value.astype(jnp.bfloat16)
    low = (value - high.astype(jnp.float32)).astype(jnp.bfloat16)
    return high, low


def dot(left, right, transposed):
    dims = (((1,), (1 if transposed else 0,)), ((), ()))
    return lax.dot_general(left, right, dims, preferred_element_type=jnp.float32)


def dot3(left, right, transposed):
    high, low = left
    return dot(high, right[0], transposed) + (dot(high, right[1], transposed) + dot(low, right[0], transposed))


def unpack_kernel(size, wide, tall, ih, il, ah, al):
    i = pl.program_id(0)
    width = ih.shape[1]
    both = wide[:, :width]
    row = i * size + lax.broadcasted_iota(jnp.int32, (size, width), 0)
    col = lax.broadcasted_iota(jnp.int32, (size, width), 1)
    ih[...], il[...] = halves(jnp.where(col <= row, both, 0.0))
    below = tall[...].T
    diagonal = wide[:, width:width + 1]
    ah[...], al[...] = halves(jnp.where(col > row, both, jnp.where(col == row, diagonal, below)))


def unpack(packed):
    width = packed.shape[0]
    size = 128
    out = jax.ShapeDtypeStruct((width, width), jnp.bfloat16)
    return pl.pallas_call(
        functools.partial(unpack_kernel, size),
        grid=(width // size,),
        out_shape=(out,) * 4,
        in_specs=[
            pl.BlockSpec((size, packed.shape[1]), lambda i: (i, 0)),
            pl.BlockSpec((width, size), lambda i: (0, i)),
        ],
        out_specs=(pl.BlockSpec((size, width), lambda i: (i, 0)),) * 4,
        compiler_params=pltpu.CompilerParams(vmem_limit_bytes=LIMIT),
        cost_estimate=pl.CostEstimate(flops=100_000_000, bytes_accessed=17_000_000, transcendentals=0),
        name="unpack",
    )(packed, packed)


def split_kernel(source, a, b, ours, theirs, ah, al, bh, bl):
    mine = source[0] == 1
    ah[...], al[...] = halves(jnp.where(mine, ours[...], a[...]))
    bh[...], bl[...] = halves(jnp.where(mine, theirs[...], b[...]))


def split(a, b, ours, theirs, source):
    rows, width = a.shape
    spec = pl.BlockSpec((128, width), lambda i, s: (i, 0))
    came = pl.BlockSpec((128, width), lambda i, s: (i * (1 - s[0]), 0))
    kept = pl.BlockSpec((128, width), lambda i, s: (i * s[0], 0))
    out = jax.ShapeDtypeStruct((rows, width), jnp.bfloat16)
    return pl.pallas_call(
        split_kernel,
        grid_spec=pltpu.PrefetchScalarGridSpec(
            num_scalar_prefetch=1,
            grid=(pl.cdiv(rows, 128),),
            in_specs=[came] * 2 + [kept] * 2,
            out_specs=(spec,) * 4,
        ),
        out_shape=(out,) * 4,
        compiler_params=pltpu.CompilerParams(vmem_limit_bytes=LIMIT),
        cost_estimate=pl.CostEstimate(flops=100_000_000, bytes_accessed=25_000_000, transcendentals=0),
        name="split",
    )(source, a, b, ours, theirs)


def columns_kernel(rows, unit, first, factor, panel, ih, il, ah, al, g, q, *corner):
    i = pl.program_id(0)
    f, p = factor[...], panel[...]
    if unit:
        row = i * TILE + lax.broadcasted_iota(jnp.int32, f.shape, 0)
        col = lax.broadcasted_iota(jnp.int32, f.shape, 1)
        f = jnp.where(row < rows, f, jnp.where(col == first[0] + row - rows, -1.0, 0.0))
        p = jnp.where(row < rows, p, 0.0)
    inverse = (ih[...], il[...])
    gg = dot3(halves(f), inverse, False)
    g[...] = gg
    z = p - dot3(halves(gg), (ah[...], al[...]), False)
    qq = dot3(halves(z), inverse, True)
    q[...] = qq
    if unit:
        corner[0][...] = qq[rows % TILE:rows % TILE + unit]


def columns(factor, panel, weights, unit=0):
    rows, width = factor.shape
    spec = pl.BlockSpec((TILE, width), lambda i, s: (i, 0))
    fixed = pl.BlockSpec((width, width), lambda i, s: (0, 0))
    out = jax.ShapeDtypeStruct((rows, width), jnp.float32)
    shapes, specs = [out, out], [spec, spec]
    if unit:
        shapes.append(jax.ShapeDtypeStruct((unit, width), jnp.float32))
        specs.append(pl.BlockSpec((unit, width), lambda i, s: (0, 0)))
    first = jnp.reshape(lax.axis_index(EVERY) * unit, (1,)).astype(jnp.int32)
    return pl.pallas_call(
        functools.partial(columns_kernel, rows, unit),
        grid_spec=pltpu.PrefetchScalarGridSpec(
            num_scalar_prefetch=1,
            grid=(pl.cdiv(rows, TILE),),
            in_specs=[spec, spec] + [fixed] * 4,
            out_specs=tuple(specs),
        ),
        out_shape=tuple(shapes),
        compiler_params=pltpu.CompilerParams(vmem_limit_bytes=LIMIT),
        cost_estimate=pl.CostEstimate(flops=18 * rows * width * width, bytes_accessed=16 * rows * width, transcendentals=0),
        name="columns",
    )(first, factor, panel, *weights)


def update_kernel(tiles, ph, plo, fh, fl, g, q, trailing, *refs):
    out = refs[-1]
    rows = ph.shape[0]
    step = 512
    gg, qq = halves(g[...]), halves(q[...])
    starts = [min(k * step, rows - step) for k in range(pl.cdiv(rows, step))]
    for s in starts:
        part = slice(s, s + step)
        u = dot3((ph[part], plo[part]), gg, True) + dot3((fh[part], fl[part]), qq, True)
        out[part] = trailing[part] - u


def update(trailing, slab, g, q, tiles, out, offset=None):
    rows, width = slab[0].shape
    fixed = pl.BlockSpec((rows, width), lambda i, t: (0, 0), pipeline_mode=pl.Buffered(1))
    tall = pl.BlockSpec((rows, TILE), lambda i, t: (0, t[i]))
    wide = pl.BlockSpec((TILE, width), lambda i, t: (i, 0))
    count = tiles.shape[0]
    if offset is not None:
        over = TILE - rows % TILE + TILE
        wide = pl.BlockSpec(
            (pl.Element(TILE, padding=(0, over)), pl.Element(width)),
            lambda i, t: (pl.multiple_of(i * TILE + t[count], 8), 0))
        tiles = jnp.concatenate([tiles, jnp.reshape(offset, (1,)).astype(jnp.int32)])
    args = [tiles, *slab, g, q, trailing]
    specs = [fixed] * 4 + [wide, wide, tall]
    alias = {}
    if out is not None:
        alias = {len(args): 0}
        args.append(out)
        specs.append(ANY)
    return pl.pallas_call(
        update_kernel,
        grid_spec=pltpu.PrefetchScalarGridSpec(
            num_scalar_prefetch=1, grid=(count,), in_specs=specs, out_specs=tall),
        out_shape=jax.ShapeDtypeStruct(trailing.shape, jnp.float32),
        input_output_aliases=alias,
        compiler_params=pltpu.CompilerParams(vmem_limit_bytes=LIMIT),
        cost_estimate=pl.CostEstimate(flops=12 * rows * width * TILE * count, bytes_accessed=12 * rows * TILE * count, transcendentals=0),
        name="update",
    )(*args)


def make_fast(ncol, devices):
    swap = [(0, 1), (1, 0)]

    def body(trailing, panel_block, factor_panel, corner_block, corner_inverse):
        rows, width = panel_block.shape
        d = lax.axis_index("depth")
        low = rows // TILE
        shift = (low + 1) * TILE - rows
        rest = rows - low * TILE

        def cut(value, first, size):
            return lax.dynamic_slice(value, (first + shift * d, 0), (size, width))

        def send(value):
            return lax.ppermute(value, "depth", swap)

        early = low - 1
        packed = pack_corner(corner_block, corner_inverse)
        theirs = send(packed)
        pair = jnp.where(d == 1, jnp.concatenate([theirs, packed], axis=0), jnp.concatenate([packed, theirs], axis=0))
        factor_first, panel_first = after((factor_panel, panel_block), pair)
        sizes = [early * TILE]
        firsts = [0]
        raw = []
        for f, s in zip(firsts, sizes):
            fc = send(cut(factor_first, f, s))
            pc = send(cut(panel_first, f, s))
            raw.append((fc, pc))

        packed, ps, fs = spread(pair, panel_first, factor_first, ncol, devices)
        weights = unpack(packed)
        source = (lax.axis_index(("row", "col")) == 0).astype(jnp.int32)
        slab = split(ps, fs, panel_block, factor_panel, jnp.reshape(source, (1,)))
        g, panel_out, corner_out = columns(factor_panel, panel_block, weights, corner_inverse.shape[0])

        done = []
        if low > early:
            done.append((early * TILE, (send(cut(g, early * TILE, TILE)), send(cut(panel_out, early * TILE, TILE)))))

        def last(value):
            high = jnp.concatenate([value[low * TILE + shift:], value[:shift]], axis=0)
            return jnp.where(d == 1, high, value[low * TILE:])

        def ids(first, count):
            return (first + jnp.arange(count)).astype(jnp.int32)

        base = d * (low + 1)
        other = (1 - d) * (low + 1)
        out = update(trailing, slab, g, panel_out, ids(base, pl.cdiv(rows - shift, TILE)), None, shift * d)
        tail = after((last(g), last(panel_out)), out)
        tail = (send(tail[0]), send(tail[1]))
        for f, s, pair in zip(firsts, sizes, raw):
            gc, qc = columns(*after(pair, out), weights)
            out = update(trailing, slab, gc, qc, ids(other + f // TILE, s // TILE), out)
        for f, pair in done:
            gc, qc = after(pair, out)
            out = update(trailing, slab, gc, qc, ids(other + f // TILE, 1), out)

        def final(value, mine):
            head = value[:rest - shift]
            end = value[rest - shift:]
            first = jnp.concatenate([head, end, mine[:shift]], axis=0)
            second = jnp.concatenate([mine[low * TILE:], end], axis=0)
            return jnp.concatenate([first, jnp.where(d == 1, first, second)], axis=0)

        tail = after(tail, out)
        last_ids = jnp.stack([jnp.where(d == 1, low, other + low), low]).astype(jnp.int32)
        out = update(trailing, slab, final(tail[0], g), final(tail[1], panel_out), last_ids, out)
        return (out, panel_out, corner_out)

    return body


def solution(mesh):
    in_specs = (
        P("depth", ("row", "col")),
        P(EVERY, None),
        P(EVERY, None),
        P(EVERY, None),
        P(EVERY, None),
    )
    out_specs = (
        P("depth", ("row", "col")),
        P(EVERY, None),
        P(EVERY, None),
    )
    layers, nrow, ncol = mesh.shape["depth"], mesh.shape["row"], mesh.shape["col"]
    general = make_general(layers)

    def body(*args):
        rows = args[1].shape[0]
        unit = args[4].shape[0]
        fits = layers == 2 and nrow == 4 and ncol > 1 and rows % 32 == 0 and rows > 2 * TILE
        fits = fits and rows % TILE + unit == TILE and unit % 8 == 0
        chosen = make_fast(ncol, layers * nrow * ncol) if fits else general
        return chosen(*args)

    return jax.shard_map(body, mesh=mesh, in_specs=in_specs, out_specs=out_specs, check_vma=False)
```

time: 482 us -> 428 us (0.89)
  the two profiles are of different devices: /device:TPU:0 before, /device:TPU:24 now
where the time goes in v1:
time: 428 us; the launch traced here: 427 us
  Pallas kernels  298 us (70%)
  waiting for transfers between devices  84.7 us (20%)
  local copies, waits for them, and re-layouts  25.3 us (6%)
  other arithmetic  11.2 us (3%)
  starting transfers between devices  7.66 us (2%)
    pallas_call x1, Pallas kernels, spread(): pl.pallas_call(functools.partial(spread_kernel, ncol, piece), out_shape=(...  115 us
    pallas_call x4, Pallas kernels, update(): pl.pallas_call(update_kernel, grid_spec=pltpu.PrefetchScalarGridSpec(num_...  96.3 us
    ppermute x7, waiting for transfers between devices, send(): return lax.ppermute(value, 'depth', swap)  84.7 us
    pallas_call x2, Pallas kernels, columns(): pl.pallas_call(functools.partial(columns_kernel, rows, unit), grid_spec=p...  62.1 us
    pallas_call x1, Pallas kernels, split(): pl.pallas_call(split_kernel, grid_spec=pltpu.PrefetchScalarGridSpec(num_s...  13.9 us
    dynamic_slice x4, local copies, waits for them, and re-layouts, cut(): return lax.dynamic_slice(value, (first + shift * d, 0), (size, width))  12.1 us
    pallas_call x1, Pallas kernels, unpack(): pl.pallas_call(functools.partial(unpack_kernel, size), grid=(width // siz...  10.4 us
    unnamed x12, local copies, waits for them, and re-layouts  8.84 us
  transfers between devices with their start and end apart: 7, of which 3 were waited for; matrix products, arithmetic and copies ran while one was open for 4% of the time, Pallas kernels for 39%

profile of v1, /device:TPU:24, one launch (start us, length us, event | category | flops | bytes accessed | tf_op | source)
XLA Modules:
  0.0 427.3 jit_solution(17495616506659979735)
XLA Ops:
  1.9 1.6 collective-permute-start
  5.4 2.2 collective-permute-done
  7.6 5.1 %constant_dynamic-slice_fusion = f32[1024,1024]{1,0:T(8,128)} fusion(f32[1504,1024]{1,0:T(8,128)} %panel.2, s32[]{:T(128)S(6)} %select_n.61), kind=kLoop, calls=%fused_computation.12 | loop fusion | bytes 8388612 | tf_op jit(solution)/shard_map/dynamic_slice | solution.py:465
  12.7 2.4 constant_dynamic-slice_fusion.1
  16.5 114.9 %spread.1 = (f32[1024,1152]{1,0:T(8,128)S(1)}, f32[1504,1024]{1,0:T(8,128)S(1)}, f32[1504,1024]{1,0:T(8,128)S(1)}) custom-call(f32[64,1152]{1,0:T(8,128)S(1)} %maximum_select_fusion.4.packed, f32[1504,1024]{1,0:T(8,128)S(1)} %bitcast.6, f32[1504,1024]{1,0:T(8,128)S(1)} %copy-done), custom_call_target="tpu_custom_call" | custom-call | flops 100000000 | bytes 40000000 | tf_op jit(solution)/shard_map/spread/pallas_call | solution.py:274
  131.5 2.2 copy-done.1
  133.7 2.7 copy-done.2
  136.3 2.6 copy-done.3
  140.9 10.4 %unpack.1 = (bf16[1024,1024]{1,0:T(8,128)(2,1)}, bf16[1024,1024]{1,0:T(8,128)(2,1)}, bf16[1024,1024]{1,0:T(8,128)(2,1)}, bf16[1024,1024]{1,0:T(8,128)(2,1)}) custom-call(f32[1024,1152]{1,0:T(8,128)} %copy-done.1, f32[1024,1152]{1,0:T(8,128)} %copy-done.1), custom_call_target="tpu_custom_call" | custom-call | flops 100000000 | bytes 17000000 | tf_op jit(solution)/shard_map/unpack/pallas_call | solution.py:326
  151.4 36.7 %columns.2 = (f32[1504,1024]{1,0:T(8,128)}, f32[1504,1024]{1,0:T(8,128)}, f32[32,1024]{1,0:T(8,128)}) custom-call(s32[1]{0:T(128)} %bitcast.2.first, f32[1504,1024]{1,0:T(8,128)} %factor.2, f32[1504,1024]{1,0:T(8,128)} %panel.2, bf16[1024,1024]{1,0:T(8,128)(2,1)} %get-tuple-element.38.ih, bf16[1024,1024]{1,0:T(8,128)(2,1)} %get-tuple-element.39.il, ...), custom_call_target="tpu_custom_call" | custom-call | flops 28387049472 | bytes 24641536 | tf_op jit(solution)/shard_map/columns/pallas_call | solution.py:396
  192.3 2.3 constant_dynamic-slice_fusion.2
  194.6 1.5 collective-permute-start.4
  196.2 2.3 constant_dynamic-slice_fusion.3
  199.0 13.9 %split.1 = (bf16[1504,1024]{1,0:T(8,128)(2,1)}, bf16[1504,1024]{1,0:T(8,128)(2,1)}, bf16[1504,1024]{1,0:T(8,128)(2,1)}, bf16[1504,1024]{1,0:T(8,128)(2,1)}) custom-call(s32[1]{0:T(128)} %bitcast.1.source, f32[1504,1024]{1,0:T(8,128)} %copy-done.2, f32[1504,1024]{1,0:T(8,128)} %copy-done.3, f32[1504,1024]{1,0:T(8,128)} %panel.2, f32[1504,1024]{1,0:T(8,128)} %factor.2), custom_call_target="tpu_custom_call" | custom-call | flops 100000000 | bytes 25000000 | tf_op jit(solution)/shard_map/split/pallas_call | solution.py:353
  212.9 2.3 fusion.1
  215.2 2.4 fusion.2
  217.6 38.4 %update.4.refs_0_ = f32[1504,3008]{1,0:T(8,128)} custom-call(s32[7]{0:T(128)} %pad_add_fusion.1.tiles, bf16[1504,1024]{1,0:T(8,128)(2,1)} %get-tuple-element.33.ph, bf16[1504,1024]{1,0:T(8,128)(2,1)} %get-tuple-element.34.plo, bf16[1504,1024]{1,0:T(8,128)(2,1)} %get-tuple-element.35.fh, bf16[1504,1024]{1,0:T(8,128)(2,1)} %get-tuple-element.36.fl, ...), custom_call_target="tpu_custom_call" | custom-call | flops 28387049472 | bytes 27721728 | tf_op jit(solution)/shard_map/update/pallas_call | solution.py:442
  258.0 64.6 %collective-permute-done.6.panel = f32[1024,1024]{1,0:T(8,128)} collective-permute-done((f32[1024,1024]{1,0:T(8,128)}, f32[1024,1024]{1,0:T(8,128)}, u32[]{:S(2)}, u32[]{:S(2)}) %collective-permute-start.6) | collective-permute-done | bytes 4194336 | tf_op jit(solution)/shard_map/ppermute | solution.py:468
  322.6 25.4 %columns.3 = (f32[1024,1024]{1,0:T(8,128)}, f32[1024,1024]{1,0:T(8,128)}) custom-call(s32[1]{0:T(128)} %constant.37.clone.1.first, f32[1024,1024]{1,0:T(8,128)} %collective-permute-done.5.factor, f32[1024,1024]{1,0:T(8,128)} %collective-permute-done.6.panel, bf16[1024,1024]{1,0:T(8,128)(2,1)} %get-tuple-element.38.ih, ...), custom_call_target="tpu_custom_call" | custom-call | flops 19327352832 | bytes 16777216 | tf_op jit(solution)/shard_map/columns/pallas_call | solution.py:396
  347.9 28.2 %update.5.refs_0_ = f32[1504,3008]{1,0:T(8,128)} custom-call(s32[4]{0:T(128)} %iota_add_fusion.tiles, bf16[1504,1024]{1,0:T(8,128)(2,1)} %get-tuple-element.33.ph, bf16[1504,1024]{1,0:T(8,128)(2,1)} %get-tuple-element.34.plo, bf16[1504,1024]{1,0:T(8,128)(2,1)} %get-tuple-element.35.fh, ...), custom_call_target="tpu_custom_call", output_to_operand_aliasing={{}: (8, {})} | custom-call | flops 18924699648 | bytes 18481152 | tf_op jit(solution)/shard_map/update/pallas_call | solution.py:442
  376.2 11.8 %update.6.refs_0_ = f32[1504,3008]{1,0:T(8,128)} custom-call(s32[1]{0:T(128)} %bitcast.4.tiles, bf16[1504,1024]{1,0:T(8,128)(2,1)} %get-tuple-element.33.ph, bf16[1504,1024]{1,0:T(8,128)(2,1)} %get-tuple-element.34.plo, bf16[1504,1024]{1,0:T(8,128)(2,1)} %get-tuple-element.35.fh, ...), custom_call_target="tpu_custom_call", output_to_operand_aliasing={{}: (8, {})} | custom-call | flops 4731174912 | bytes 4620288 | tf_op jit(solution)/shard_map/update/pallas_call | solution.py:442
  387.9 18.0 %collective-permute-done.2 = f32[224,1024]{1,0:T(8,128)S(1)} collective-permute-done((f32[224,1024]{1,0:T(8,128)}, f32[224,1024]{1,0:T(8,128)S(1)}, u32[]{:S(2)}, u32[]{:S(2)}) %collective-permute-start.2) | collective-permute-done | bytes 917536 | tf_op jit(solution)/shard_map/ppermute | solution.py:468
  406.3 1.5 pad_maximum_fusion.g
  409.3 18.0 %update.7 = f32[1504,3008]{1,0:T(8,128)} custom-call(s32[2]{0:T(128)} %pad_add_fusion.tiles, bf16[1504,1024]{1,0:T(8,128)(2,1)} %get-tuple-element.33.ph, bf16[1504,1024]{1,0:T(8,128)(2,1)} %get-tuple-element.34.plo, bf16[1504,1024]{1,0:T(8,128)(2,1)} %get-tuple-element.35.fh, ...), custom_call_target="tpu_custom_call", output_to_operand_aliasing={{}: (8, {})} | custom-call | flops 9462349824 | bytes 9240576 | tf_op jit(solution)/shard_map/update/pallas_call | solution.py:442
  (36 shorter events, 15.3 us)
Async XLA Ops:
  1.9 5.7 %collective-permute-start = (f32[32,1152]{1,0:T(8,128)S(1)}, f32[32,1152]{1,0:T(8,128)S(1)}, u32[]{:S(2)}, u32[]{:S(2)}) collective-permute-start(f32[32,1152]{1,0:T(8,128)S(1)} %pad_maximum_fusion.2), channel_id=1, source_target_pairs={{0,1},{1,0},{2,3},{3,2},{4,5},{5,4},{6,7},{7,6},{8,9},{9,8},{10,11... | collective-permute-start | bytes 442376 | tf_op jit(solution)/shard_map/ppermute | solution.py:468
  7.6 5.1 %copy-start = (f32[1504,1024]{1,0:T(8,128)S(1)}, f32[1504,1024]{1,0:T(8,128)}, u32[]{:S(2)}) copy-start(f32[1504,1024]{1,0:T(8,128)} %factor.2) | copy-start | bytes 18481156
  7.6 7.5 %slice-start = ((s8[6160384]{0:T(1024)(128)(4,1)}), s8[4194304]{0:T(1024)(128)(4,1)S(1)}, s32[]{:S(2)}) async-start(s8[6160384]{0:T(1024)(128)(4,1)} %bitcast.5), calls=%async_computation | async-start | bytes 8388608
  12.7 3.8 slice-start.1
  131.5 2.2 copy-start.1
  133.7 2.7 copy-start.2
  136.3 2.6 copy-start.3
  138.9 118.5 %collective-permute-start.5 = (f32[1024,1024]{1,0:T(8,128)}, f32[1024,1024]{1,0:T(8,128)}, u32[]{:S(2)}, u32[]{:S(2)}) collective-permute-start(f32[1024,1024]{1,0:T(8,128)} %constant_dynamic-slice_fusion.1), channel_id=1, source_target_pairs={{0,1},{1,0},{2,3},{3,2},{4,5},{5,4},{6,7},{7,6},{8,9},{9,8},{10,11... | collective-permute-start | bytes 12582920 | tf_op jit(solution)/shard_map/ppermute | solution.py:468
  140.4 182.1 %collective-permute-start.6 = (f32[1024,1024]{1,0:T(8,128)}, f32[1024,1024]{1,0:T(8,128)}, u32[]{:S(2)}, u32[]{:S(2)}) collective-permute-start(f32[1024,1024]{1,0:T(8,128)} %constant_dynamic-slice_fusion), channel_id=1, source_target_pairs={{0,1},{1,0},{2,3},{3,2},{4,5},{5,4},{6,7},{7,6},{8,9},{9,8},{10,11... | collective-permute-start | bytes 12582920 | tf_op jit(solution)/shard_map/ppermute | solution.py:468
  194.6 181.5 %collective-permute-start.4 = (f32[256,1024]{1,0:T(8,128)}, f32[256,1024]{1,0:T(8,128)}, u32[]{:S(2)}, u32[]{:S(2)}) collective-permute-start(f32[256,1024]{1,0:T(8,128)} %constant_dynamic-slice_fusion.2), channel_id=1, source_target_pairs={{0,1},{1,0},{2,3},{3,2},{4,5},{5,4},{6,7},{7,6},{8,9},{9,8},{10,11... | collective-permute-start | bytes 3145736 | tf_op jit(solution)/shard_map/ppermute | solution.py:468
  198.5 177.7 %collective-permute-start.3 = (f32[256,1024]{1,0:T(8,128)}, f32[256,1024]{1,0:T(8,128)}, u32[]{:S(2)}, u32[]{:S(2)}) collective-permute-start(f32[256,1024]{1,0:T(8,128)} %constant_dynamic-slice_fusion.3), channel_id=1, source_target_pairs={{0,1},{1,0},{2,3},{3,2},{4,5},{5,4},{6,7},{7,6},{8,9},{9,8},{10,11... | collective-permute-start | bytes 3145736 | tf_op jit(solution)/shard_map/ppermute | solution.py:468
  256.0 132.0 %collective-permute-start.1 = (f32[224,1024]{1,0:T(8,128)}, f32[224,1024]{1,0:T(8,128)S(1)}, u32[]{:S(2)}, u32[]{:S(2)}) collective-permute-start(f32[224,1024]{1,0:T(8,128)} %get-tuple-element.44), channel_id=1, source_target_pairs={{0,1},{1,0},{2,3},{3,2},{4,5},{5,4},{6,7},{7,6},{8,9},{9,8},{10,11... | collective-permute-start | bytes 2752520 | tf_op jit(solution)/shard_map/ppermute | solution.py:468
  257.5 148.4 %collective-permute-start.2 = (f32[224,1024]{1,0:T(8,128)}, f32[224,1024]{1,0:T(8,128)S(1)}, u32[]{:S(2)}, u32[]{:S(2)}) collective-permute-start(f32[224,1024]{1,0:T(8,128)} %get-tuple-element.45), channel_id=1, source_target_pairs={{0,1},{1,0},{2,3},{3,2},{4,5},{5,4},{6,7},{7,6},{8,9},{9,8},{10,11... | collective-permute-start | bytes 2752520 | tf_op jit(solution)/shard_map/ppermute | solution.py:468

commit v2 on v0

v2 whole, which is shorter than its diff:
```python
import functools

import jax
import jax.numpy as jnp
from jax import lax
from jax.experimental import pallas as pl
from jax.experimental.pallas import tpu as pltpu
from jax.sharding import PartitionSpec as P


EVERY = ("row", "col", "depth")
MESH = pl.DeviceIdType.MESH
TILE = 256
LIMIT = 60 * 1024 * 1024
ANY = pl.BlockSpec(memory_space=pl.ANY)


def matmul(left, right):
    return jnp.dot(left, right, precision=lax.Precision.HIGH, preferred_element_type=jnp.float32)


def contract(left, right):
    return lax.dot_general(
        left,
        right,
        (((1,), (1,)), ((), ())),
        precision=lax.Precision.HIGH,
        preferred_element_type=jnp.float32,
    )


def pack_corner(corner_block, corner_inverse):
    rows, width = corner_inverse.shape
    first = lax.axis_index(EVERY) * rows
    row = first + lax.broadcasted_iota(jnp.int32, (rows, width), 0)
    col = lax.broadcasted_iota(jnp.int32, (rows, width), 1)
    both = jnp.where(col > row, corner_block, corner_inverse)
    diagonal = jnp.sum(jnp.where(col == row, corner_block, 0.0), axis=1, keepdims=True)
    return jnp.concatenate([both, jnp.broadcast_to(diagonal, (rows, 128))], axis=1)


def unpack_corner(packed, width):
    row = lax.broadcasted_iota(jnp.int32, (width, width), 0)
    col = lax.broadcasted_iota(jnp.int32, (width, width), 1)
    both = packed[:, :width]
    inverse = jnp.where(col <= row, both, 0.0)
    upper = jnp.where(col > row, both, jnp.where(col == row, 0.5 * packed[:, width:width + 1], 0.0))
    return inverse, upper


def transform(panel, factor, inverse, corner):
    coupling = matmul(factor, corner)
    half = contract(panel, inverse) - 0.5 * coupling
    return half - 0.5 * coupling


def exchange(value, layers):
    blocks = [value]
    for shift in range(1, layers):
        pairs = [(source, (source + shift) % layers) for source in range(layers)]
        blocks.append(lax.ppermute(value, "depth", pairs))
    return blocks


def arrange(blocks, layers):
    if layers == 1:
        return blocks[0]
    me = lax.axis_index("depth")
    rows, width = blocks[0].shape
    whole = jnp.zeros((layers * rows, width), blocks[0].dtype)
    for shift, block in enumerate(blocks):
        place = lax.rem(me - shift + layers, layers)
        whole = lax.dynamic_update_slice(whole, block, (place * rows, 0))
    return whole


def make_general(layers):
    def body(trailing, panel_block, factor_panel, corner_block, corner_inverse):
        rows, width = panel_block.shape
        factor_blocks = exchange(factor_panel, layers)
        panel_blocks = exchange(panel_block, layers)
        packed = lax.all_gather(pack_corner(corner_block, corner_inverse), EVERY, axis=0, tiled=True)
        source = lax.axis_index(("row", "col")) == 0
        kept = jnp.where(source, jnp.concatenate((panel_block, factor_panel), axis=0), 0.0)
        slab = lax.psum(kept, ("row", "col"))
        inverse, upper = unpack_corner(packed, width)
        triangle = matmul(inverse, contract(upper, inverse))
        corner = triangle + triangle.T
        corner_rows = corner_inverse.shape[0]
        corner_out = lax.dynamic_slice(
            corner, (lax.axis_index(EVERY) * corner_rows, 0), (corner_rows, width)
        )
        panel_out = transform(panel_block, factor_panel, inverse, corner)
        factor_cols = arrange(factor_blocks, layers)
        panel_cols = arrange(panel_blocks, layers)
        left = transform(slab[:rows], slab[rows:], inverse, corner)
        right = matmul(slab[rows:], inverse)
        trailing_out = (trailing - contract(left, factor_cols)) - contract(right, panel_cols)
        return (trailing_out, panel_out, corner_out)

    return body


def after(value, earlier):
    return lax.optimization_barrier((value, earlier))[0]


def halves(value):
    high = value.astype(jnp.bfloat16)
    low = (value - high.astype(jnp.float32)).astype(jnp.bfloat16)
    return high, low


def dot(left, right, transposed):
    dims = (((1,), (1 if transposed else 0,)), ((), ()))
    return lax.dot_general(left, right, dims, preferred_element_type=jnp.float32)


def dot3(left, right, transposed):
    high, low = left
    return dot(high, right[0], transposed) + (dot(high, right[1], transposed) + dot(low, right[0], transposed))


def column_tile(f, p, ih, il, ah, al):
    width = f.shape[1]
    fh, fl = halves(f)
    gs = []
    for j in range(0, width, TILE):
        w = (ih[j:, j:j + TILE], il[j:, j:j + TILE])
        gs.append(dot3((fh[:, j:], fl[:, j:]), w, False))
    g = jnp.concatenate(gs, axis=1)
    z = p - dot3(halves(g), (ah[...], al[...]), False)
    zh, zl = halves(z)
    qs = []
    for j in range(TILE, width + TILE, TILE):
        w = (ih[j - TILE:j, :j], il[j - TILE:j, :j])
        qs.append(dot3((zh[:, :j], zl[:, :j]), w, True))
    return g, jnp.concatenate(qs, axis=1)


def spread_kernel(ncol, piece, packed, panel, factor,
                  ps, fs, ih_out, il_out, ah_out, al_out, g_out, q_out, corner_out, *more):
    (gs2, gs3, gtop, gend, qs2, qs3, qtop, qend,
     corner, ih, il, ah, al, fbuf, pbuf, gbuf, qbuf,
     yl, zr, zl, xr, cr, sz, sx, sc, rm, rp, su, sd, sq, loads, saves) = more
    r, c, d = lax.axis_index("row"), lax.axis_index("col"), lax.axis_index("depth")
    x, core = r // 2, r % 2
    across, mate = (1 - x) * 2 + core, x * 2 + (1 - core)
    block = packed.shape[0]
    rows, width = ps.shape
    count = rows // piece
    source = (r == 0) & (c == 0)

    def at(ref, first, size):
        return ref.at[pl.ds(pl.multiple_of(first, 8), size)]

    def remote(src, dst, send, recv, row, col, depth):
        return pltpu.make_async_remote_copy(
            src_ref=src, dst_ref=dst, send_sem=send, recv_sem=recv,
            device_id=(row, col, depth), device_id_type=MESH)

    keep = pltpu.make_async_copy(packed, at(corner, (r * ncol + c) * block, block), yl)
    keep.start()
    keep.wait()

    def rows_of(row, col):
        return at(corner, (row * ncol + col) * block, block)

    def forward_line(col, right, left):
        b = rows_of(r, col)

        if right:
            @pl.when(c < ncol - 1)
            def _():
                remote(b, b, sz.at[0, col], zr.at[col], r, c + 1, d).start()
        if left:
            @pl.when(c > 0)
            def _():
                remote(b, b, sz.at[1, col], zl.at[col], r, c - 1, d).start()
        remote(b, b, sx.at[col], xr.at[col], across, c, d).start()
        remote(b, b, sc.at[0, col], cr.at[0, col], mate, c, d).start()

    forward_line(c, True, True)

    load_f = pltpu.make_async_copy(factor, fbuf.at[:rows], loads.at[0])
    load_p = pltpu.make_async_copy(panel, pbuf.at[:rows], loads.at[1])
    load_f.start()
    load_p.start()

    trunk = x == core
    notsource = jnp.logical_not(source)
    up = trunk & (c < ncol - 1) & notsource
    side = trunk & (c > 0)
    down = (core == 0) & (x == 1) & (c == 1)
    local = (x > 0) | (c > 0)
    near = c == 0
    hops = jnp.where(core == 0, jnp.where(x == 0, c, jnp.where(near, 3, c + 1)),
                     jnp.where(x == 1, c + 1, jnp.where(near, 1, c + 2)))
    group = 3

    def pass_on(ref, j):
        def step(n, carry):
            k = j * group + n

            @pl.when(k < count)
            def _():
                v = ref.at[pl.ds(pl.multiple_of(k * piece, 8), piece)]
                remote(v, v, su, rm.at[k], r, c, d).wait_recv()

                @pl.when(up)
                def _():
                    remote(v, v, su, rm.at[k], r, c + 1, d).start()

                @pl.when(side)
                def _():
                    remote(v, v, sd, rm.at[k], across, c, d).start()

                @pl.when(down)
                def _():
                    remote(v, v, sd, rm.at[k], r, 0, d).start()

                @pl.when(local)
                def _():
                    remote(v, v, sq.at[0], rp, mate, c, d).start()

            return carry

        lax.fori_loop(0, group, step, 0)

    def begin(j):
        def step(n, carry):
            k = j * group + n

            @pl.when(k < count)
            def _():
                s = pl.ds(pl.multiple_of(k * piece, 8), piece)
                remote(factor.at[s], fs.at[s], su, rm.at[k], 0, 1, d).start()
                remote(panel.at[s], ps.at[s], sd, rm.at[k], 3, 0, d).start()
                remote(factor.at[s], fs.at[s], sq.at[0], rp, 1, 0, d).start()
                remote(panel.at[s], ps.at[s], sq.at[1], rm.at[k], 1, 0, d).start()

            return carry

        lax.fori_loop(0, group, step, 0)

    def position(i):
        @pl.when(source & (i * group < count))
        def _():
            begin(i)

        j = i - hops
        due = notsource & (j >= 0) & (j * group < count)

        @pl.when(due & (core == 0))
        def _():
            pass_on(fs, j)

        @pl.when(due & (core == 1))
        def _():
            pass_on(ps, j)

    done = 0
    position(done)
    for s in range(1, ncol):
        @pl.when(c - s >= 0)
        def _():
            b = rows_of(r, c - s)
            remote(b, b, sz.at[0, c - s], zr.at[c - s], r, c, d).wait_recv()
            forward_line(c - s, True, False)

        @pl.when(c + s < ncol)
        def _():
            b = rows_of(r, c + s)
            remote(b, b, sz.at[1, c + s], zl.at[c + s], r, c, d).wait_recv()
            forward_line(c + s, False, True)

        done += 1
        position(done)

    def across_block(col):
        b = rows_of(across, col)
        remote(b, b, sx.at[col], xr.at[col], across, c, d).wait_recv()
        remote(b, b, sc.at[1, col], cr.at[1, col], mate, c, d).start()

    across_block(c)
    done += 1
    position(done)
    for s in range(1, ncol):
        @pl.when(c - s >= 0)
        def _():
            across_block(c - s)

        @pl.when(c + s < ncol)
        def _():
            across_block(c + s)

        done += 1
        position(done)

    for col in range(ncol):
        for half in range(2):
            b = rows_of(0, col)
            remote(b, b, sc.at[half, col], cr.at[half, col], mate, c, d).wait()
        remote(b, b, sx.at[col], rp, r, c, d).wait_send()

        @pl.when((c < ncol - 1) & (col <= c))
        def _():
            b = rows_of(0, col)
            remote(b, b, sz.at[0, col], rp, r, c, d).wait_send()

        @pl.when((c > 0) & (col >= c))
        def _():
            b = rows_of(0, col)
            remote(b, b, sz.at[1, col], rp, r, c, d).wait_send()

    size = 128

    def unpack_step(i, carry):
        part = pl.ds(pl.multiple_of(i * size, size), size)
        wide = corner[part, :]
        both = wide[:, :width]
        row = i * size + lax.broadcasted_iota(jnp.int32, (size, width), 0)
        col = lax.broadcasted_iota(jnp.int32, (size, width), 1)
        ih[part, :], il[part, :] = halves(jnp.where(col <= row, both, 0.0))
        below = corner[:, part].T
        diagonal = wide[:, width:width + 1]
        ah[part, :], al[part, :] = halves(jnp.where(col > row, both, jnp.where(col == row, diagonal, below)))

        @pl.when(i % 2 == 1)
        def _():
            position(done + 1 + i // 2)

        return carry

    lax.fori_loop(0, width // size, unpack_step, 0)
    done += width // size // 2

    load_f.wait()
    load_p.wait()
    unit = fbuf.shape[0] - rows
    fbuf[rows:] = jnp.zeros((unit, width), jnp.float32)
    pbuf[rows:] = jnp.zeros((unit, width), jnp.float32)
    first = ((r * ncol + c) * 2 + d) * unit
    tiles = fbuf.shape[0] // TILE

    def columns_step(i, carry):
        part = pl.ds(pl.multiple_of(i * TILE, TILE), TILE)
        row = i * TILE + lax.broadcasted_iota(jnp.int32, (TILE, width), 0)
        col = lax.broadcasted_iota(jnp.int32, (TILE, width), 1)
        f = jnp.where(row < rows, fbuf[part, :], jnp.where(col == first + row - rows, -1.0, 0.0))
        gbuf[part, :], qbuf[part, :] = column_tile(f, pbuf[part, :], ih, il, ah, al)
        position(done + 1 + i)
        return carry

    lax.fori_loop(0, tiles, columns_step, 0)
    done += tiles

    outs = [
        pltpu.make_async_copy(gbuf.at[:rows], g_out, saves.at[0]),
        pltpu.make_async_copy(qbuf.at[:rows], q_out, saves.at[1]),
        pltpu.make_async_copy(qbuf.at[rows:], corner_out, saves.at[2]),
        pltpu.make_async_copy(ih, ih_out, saves.at[3]),
        pltpu.make_async_copy(il, il_out, saves.at[4]),
        pltpu.make_async_copy(ah, ah_out, saves.at[5]),
        pltpu.make_async_copy(al, al_out, saves.at[6]),
    ]
    low = rows // TILE
    cut = rows - gs3.shape[0] - gs2.shape[0]
    for buf, outs4 in ((gbuf, (gs2, gs3, gtop, gend)), (qbuf, (qs2, qs3, qtop, qend))):
        firsts = (cut, cut + gs2.shape[0], 0, low * TILE)
        for start, out in zip(firsts, outs4):
            outs.append(pltpu.make_async_copy(buf.at[start:start + out.shape[0]], out, saves.at[len(outs)]))
    for copy in outs:
        copy.start()

    last = pl.cdiv(count, group) + ncol + 1

    def rest(i, carry):
        position(i)
        return carry

    lax.fori_loop(done + 1, max(last, done + 1), rest, 0)

    @pl.when(notsource)
    def _():
        remote(ps, ps, su, rp, r, c, d).wait_recv()

        @pl.when(up)
        def _():
            remote(ps, ps, su, rp, r, c, d).wait_send()

        @pl.when(side | down)
        def _():
            remote(ps, ps, sd, rp, r, c, d).wait_send()

        @pl.when(local)
        def _():
            remote(ps, ps, sq.at[0], rp, r, c, d).wait_send()

    @pl.when(source)
    def _():
        for sem in (su, sd, sq.at[0], sq.at[1]):
            remote(ps, ps, sem, rp, r, c, d).wait_send()

    for copy in outs:
        copy.wait()


def spread(packed, panel, factor, unit, sizes, ncol, devices):
    rows, width = panel.shape
    piece = 32
    count = rows // piece
    dma = pltpu.SemaphoreType.DMA
    hbm = pl.BlockSpec(memory_space=pltpu.HBM)
    weight = (width, width)
    tall = (rows + unit, width)
    return pl.pallas_call(
        functools.partial(spread_kernel, ncol, piece),
        out_shape=tuple(
            [jax.ShapeDtypeStruct(panel.shape, jnp.float32)] * 2
            + [jax.ShapeDtypeStruct(weight, jnp.bfloat16)] * 4
            + [jax.ShapeDtypeStruct(panel.shape, jnp.float32)] * 2
            + [jax.ShapeDtypeStruct((n, width), jnp.float32) for n in (unit,) + sizes * 2]
        ),
        in_specs=[hbm] * 3,
        out_specs=(hbm,) * 17,
        scratch_shapes=[
            pltpu.VMEM((packed.shape[0] * devices // 2, packed.shape[1]), jnp.float32),
            *[pltpu.VMEM(weight, jnp.bfloat16)] * 4,
            *[pltpu.VMEM(tall, jnp.float32)] * 4,
            dma, dma((ncol,)), dma((ncol,)), dma((ncol,)), dma((2, ncol)),
            dma((2, ncol)), dma((ncol,)), dma((2, ncol)),
            dma((count,)), dma, dma, dma, dma((2,)), dma((2,)), dma((15,)),
        ],
        compiler_params=pltpu.CompilerParams(has_side_effects=True, vmem_limit_bytes=LIMIT),
        cost_estimate=pl.CostEstimate(flops=18 * rows * width * width, bytes_accessed=40_000_000, transcendentals=0),
        name="spread",
    )(packed, panel, factor)


def split_kernel(source, a, b, ours, theirs, q, out, kept):
    kept[...] = q[...]
    mine = source[0] == 1
    width = a.shape[1]
    out[:, width:2 * width], out[:, :width] = halves(jnp.where(mine, ours[...], a[...]))
    out[:, 2 * width:3 * width], out[:, 3 * width:] = halves(jnp.where(mine, theirs[...], b[...]))


def split(a, b, ours, theirs, q, source):
    rows, width = a.shape
    came = pl.BlockSpec((TILE, width), lambda i, s: (i * (1 - s[0]), 0))
    kept = pl.BlockSpec((TILE, width), lambda i, s: (i * s[0], 0))
    return pl.pallas_call(
        split_kernel,
        grid_spec=pltpu.PrefetchScalarGridSpec(
            num_scalar_prefetch=1,
            grid=(pl.cdiv(rows, TILE),),
            in_specs=[came] * 2 + [kept] * 2 + [pl.BlockSpec((TILE, width), lambda i, s: (i, 0))],
            out_specs=tuple(pl.BlockSpec((TILE, n), lambda i, s: (i, 0)) for n in (4 * width, width)),
        ),
        out_shape=(jax.ShapeDtypeStruct((rows, 4 * width), jnp.bfloat16), jax.ShapeDtypeStruct(q.shape, jnp.float32)),
        compiler_params=pltpu.CompilerParams(vmem_limit_bytes=LIMIT),
        cost_estimate=pl.CostEstimate(flops=100_000_000, bytes_accessed=25_000_000, transcendentals=0),
        name="split",
    )(source, a, b, ours, theirs, q)


def columns_kernel(factor, panel, ih, il, ah, al, g, q):
    g[...], q[...] = column_tile(factor[...], panel[...], ih, il, ah, al)


def columns(factor, panel, weights):
    rows, width = factor.shape
    spec = pl.BlockSpec((TILE, width), lambda i: (i, 0))
    fixed = pl.BlockSpec((width, width), lambda i: (0, 0))
    out = jax.ShapeDtypeStruct((rows, width), jnp.float32)
    return pl.pallas_call(
        columns_kernel,
        grid=(pl.cdiv(rows, TILE),),
        in_specs=[spec, spec] + [fixed] * 4,
        out_specs=(spec, spec),
        out_shape=(out, out),
        compiler_params=pltpu.CompilerParams(vmem_limit_bytes=LIMIT),
        cost_estimate=pl.CostEstimate(flops=18 * rows * width * width, bytes_accessed=16 * rows * width, transcendentals=0),
        name="columns",
    )(factor, panel, *weights)


def update_kernel(tiles, slab, g, q, trailing, *refs):
    out, full, half = refs[-3:]
    width = g.shape[1]

    @pl.when(pl.program_id(1) == 0)
    def _():
        gh, half[:, :width] = halves(g[...])
        qh, half[:, width:] = halves(q[...])
        full[:, :width] = gh
        full[:, width:2 * width] = gh
        full[:, 2 * width:3 * width] = qh
        full[:, 3 * width:] = qh

    u = dot(slab[...], full[...], True) + dot(slab[:, width:3 * width], half[...], True)
    out[...] = trailing[...] - u


def update(trailing, slab, g, q, tiles, out, offset=None, tile=TILE):
    rows, width = slab.shape[0], g.shape[1]
    step = 512
    count = tiles.shape[0]
    part = pl.BlockSpec((step, 4 * width), lambda i, j, t: (j, 0))
    tall = pl.BlockSpec((step, tile), lambda i, j, t: (j, t[i]))
    wide = pl.BlockSpec((tile, width), lambda i, j, t: (i, 0))
    if offset is not None:
        over = 2 * tile
        wide = pl.BlockSpec(
            (pl.Element(tile, padding=(0, over)), pl.Element(width)),
            lambda i, j, t: (pl.multiple_of(i * tile + t[count], 8), 0))
        tiles = jnp.concatenate([tiles, jnp.reshape(offset, (1,)).astype(jnp.int32)])
    args = [tiles, slab, g, q, trailing]
    specs = [part, wide, wide, tall]
    alias = {}
    if out is not None:
        alias = {len(args): 0}
        args.append(out)
        specs.append(ANY)
    return pl.pallas_call(
        update_kernel,
        grid_spec=pltpu.PrefetchScalarGridSpec(
            num_scalar_prefetch=1, grid=(count, pl.cdiv(rows, step)), in_specs=specs, out_specs=tall,
            scratch_shapes=[pltpu.VMEM((tile, 4 * width), jnp.bfloat16), pltpu.VMEM((tile, 2 * width), jnp.bfloat16)]),
        out_shape=jax.ShapeDtypeStruct(trailing.shape, jnp.float32),
        input_output_aliases=alias,
        compiler_params=pltpu.CompilerParams(vmem_limit_bytes=LIMIT),
        cost_estimate=pl.CostEstimate(flops=12 * rows * width * tile * count, bytes_accessed=12 * rows * tile * count, transcendentals=0),
        name="update",
    )(*args)


def make_fast(ncol, devices):
    swap = [(0, 1), (1, 0)]

    def body(trailing, panel_block, factor_panel, corner_block, corner_inverse):
        rows, _ = panel_block.shape
        d = lax.axis_index("depth")
        low = rows // TILE
        shift = (low + 1) * TILE - rows

        def send(value):
            return lax.ppermute(value, "depth", swap)

        early = low - 1
        first = early * TILE + shift
        packed = pack_corner(corner_block, corner_inverse)
        theirs = send(packed)
        pair = jnp.where(d == 1, jnp.concatenate([theirs, packed], axis=0), jnp.concatenate([packed, theirs], axis=0))
        factor_raw = send(factor_panel[:first])
        panel_raw = send(panel_block[:first])

        sent = (TILE, rows - first - TILE, shift, rows - low * TILE)
        ps, fs, *more = spread(pair, panel_block, factor_panel, corner_inverse.shape[0], sent, ncol, devices)
        weights, (g, q, corner_out) = more[:4], more[4:7]
        ends = more[7:11], more[11:]
        source = (lax.axis_index(("row", "col")) == 0).astype(jnp.int32)
        slab, panel_out = split(ps, fs, panel_block, factor_panel, q, jnp.reshape(source, (1,)))

        def ids(first, count):
            return (first + jnp.arange(count)).astype(jnp.int32)

        base = d * (low + 1)
        other = (1 - d) * (low + 1)
        size = 2 * TILE if (low + 1) % 2 == 0 and early % 2 == 0 else TILE
        second = []
        for v in ends:
            second.append(send(v[0]))

        out = update(trailing, slab, g, q, ids(base * TILE // size, pl.cdiv(rows - shift, size)), None, shift * d, size)
        third = [send(v) for v in after([v[1] for v in ends], out)]

        early_cols = columns(*after((factor_raw, panel_raw), out), weights)
        out = update(trailing, slab, *early_cols, ids(other * TILE // size, early * TILE // size), out, shift * (1 - d), size)

        def middle(have, came, mine):
            ahead = jnp.concatenate([have[early * TILE:], came[:TILE - shift]], axis=0)
            across = jnp.concatenate([mine[3], have[:shift]], axis=0)
            return jnp.concatenate([jnp.where(d == 1, ahead, came), jnp.where(d == 1, ahead, across)], axis=0)

        second = after(second, out)
        cols = [middle(*v) for v in zip(early_cols, second, ends)]
        out = update(trailing, slab, *cols, jnp.stack([other + early, jnp.where(d == 1, early, low)]).astype(jnp.int32), out)

        def final(came, end, mine):
            ahead = jnp.concatenate([came[TILE - shift:], end, mine[2]], axis=0)
            return jnp.where(d == 1, ahead, jnp.concatenate([end, came[:TILE - end.shape[0]]], axis=0))

        third = after(third, out)
        cols = [final(*v) for v in zip(second, third, ends)]
        out = update(trailing, slab, *cols, ids(other + low, 1), out)
        return (out, panel_out, corner_out)

    return body


def solution(mesh):
    in_specs = (
        P("depth", ("row", "col")),
        P(EVERY, None),
        P(EVERY, None),
        P(EVERY, None),
        P(EVERY, None),
    )
    out_specs = (
        P("depth", ("row", "col")),
        P(EVERY, None),
        P(EVERY, None),
    )
    layers, nrow, ncol = mesh.shape["depth"], mesh.shape["row"], mesh.shape["col"]
    general = make_general(layers)

    def body(*args):
        rows = args[1].shape[0]
        unit = args[4].shape[0]
        fits = layers == 2 and nrow == 4 and ncol > 1 and rows % 32 == 0 and rows > 4 * TILE and args[1].shape[1] % TILE == 0
        fits = fits and rows % TILE + unit == TILE and unit % 8 == 0
        chosen = make_fast(ncol, layers * nrow * ncol) if fits else general
        return chosen(*args)

    return jax.shard_map(body, mesh=mesh, in_specs=in_specs, out_specs=out_specs, check_vma=False)
```

time: 482 us -> 295 us (0.61); the launches traced: 477 us -> 295 us
  Pallas kernels: 0 us -> 237 us
  waiting for transfers between devices: 235 us -> 24.3 us
  matrix products: 160 us -> 0 us
  local copies, waits for them, and re-layouts: 41.7 us -> 13.4 us
  between operations: 16.1 us -> 0.85 us
  other arithmetic: 20.4 us -> 10.6 us
  starting transfers between devices: 3.22 us -> 9.14 us
    pallas_call x0 -> x7, Pallas kernels: none -> 237 us  [the longest x1 99 us: spread(): pl.pallas_call(functools.partial(spread_kernel, ncol, piece), out_shape=t...]
    ppermute x2 -> x7, waiting for transfers between devices: 235 us -> 24.3 us  [send(): return lax.ppermute(value, 'depth', swap)]
    dot_general x9 -> x0, matrix products: 160 us -> none  [the longest x5 115 us: contract(): lax.dot_general(left, right, (((1,), (1,)), ((), ())), precision=lax.Prec...]
    dynamic_update_slice x4 -> x0, local copies, waits for them, and re-layouts: 23.4 us -> none  [arrange(): whole = lax.dynamic_update_slice(whole, block, (place * rows, 0))]
    broadcast_in_dim x3 -> x1, local copies, waits for them, and re-layouts: 12 us -> 0.07 us  [pack_corner(): jnp.broadcast_to(diagonal, (rows, 128))]
    slice x0 -> x15, local copies, waits for them, and re-layouts: none -> 10.7 us  [the longest x1 4.8 us: body(): factor_raw = send(factor_panel[:first])]
    select_n x2 -> x5, other arithmetic: 13.3 us -> 5.74 us  [the longest x1 3.29 us: final(): jnp.where(d == 1, ahead, jnp.concatenate([end, came[:TILE - end.shape[0]]...]
    ppermute x2 -> x7, starting transfers between devices: 3.14 us -> 9.14 us  [send(): return lax.ppermute(value, 'depth', swap)]
  transfers between devices with their start and end apart: 4 -> 7, of which waited for: 2 -> 1; matrix products, arithmetic and copies ran while one was open for 22% -> 5% of each run, Pallas kernels for 0% -> 77%
where the time goes in v2:
time: 295 us
  Pallas kernels  237 us (80%)
  waiting for transfers between devices  24.3 us (8%)
  local copies, waits for them, and re-layouts  13.4 us (5%)
  other arithmetic  10.6 us (4%)
  starting transfers between devices  9.14 us (3%)
    pallas_call x1, Pallas kernels, spread(): pl.pallas_call(functools.partial(spread_kernel, ncol, piece), out_shape=t...  99 us
    pallas_call x4, Pallas kernels, update(): pl.pallas_call(update_kernel, grid_spec=pltpu.PrefetchScalarGridSpec(num_...  96.9 us
    pallas_call x1, Pallas kernels, columns(): pl.pallas_call(columns_kernel, grid=(pl.cdiv(rows, TILE),), in_specs=[spe...  25.7 us
    ppermute x7, waiting for transfers between devices, send(): return lax.ppermute(value, 'depth', swap)  24.3 us
    pallas_call x1, Pallas kernels, split(): pl.pallas_call(split_kernel, grid_spec=pltpu.PrefetchScalarGridSpec(num_s...  15 us
    ppermute x7, starting transfers between devices, send(): return lax.ppermute(value, 'depth', swap)  9.14 us
  transfers between devices with their start and end apart: 7, of which 1 were waited for; matrix products, arithmetic and copies ran while one was open for 5% of the time, Pallas kernels for 77%

profile of v2, /device:TPU:0, one launch (start us, length us, event | category | flops | bytes accessed | tf_op | source)
XLA Modules:
  0.0 294.7 jit_solution(6716035485778263364)
XLA Ops:
  0.7 1.2 fusion.2
  1.9 3.1 %collective-permute-start = (f32[32,1152]{1,0:T(8,128)S(1)}, f32[32,1152]{1,0:T(8,128)S(1)}, u32[]{:S(2)}, u32[]{:S(2)}) collective-permute-start(f32[32,1152]{1,0:T(8,128)S(1)} %pad_maximum_fusion.4), channel_id=1, source_target_pairs={{0,1},{1,0},{2,3},{3,2},{4,5},{5,4},{6,7},{7,6},{8,9},{9,8},{10,11... | collective-permute-start | bytes 442376 | tf_op jit(solution)/shard_map/ppermute | solution.py:549
  5.0 4.8 %slice.36 = f32[1056,1024]{1,0:T(8,128)} slice(f32[1504,1024]{1,0:T(8,128)} %theirs.1), slice={[0:1056], [0:1024]} | slice | bytes 8650752 | tf_op jit(solution)/shard_map/slice | solution.py:556
  10.0 2.4 slice.37
  12.4 1.9 collective-permute-start.4
  15.5 0.7 pad_add_fusion.2.tiles
  16.2 0.7 maximum_select_fusion.4.packed
  16.9 99.0 %spread.1 = (f32[1504,1024]{1,0:T(8,128)}, f32[1504,1024]{1,0:T(8,128)}, bf16[1024,1024]{1,0:T(8,128)(2,1)}, bf16[1024,1024]{1,0:T(8,128)(2,1)}, bf16[1024,1024]...) custom-call(f32[64,1152]{1,0:T(8,128)} %maximum_select_fusion.4.pack, ...), custom_call_target="tpu_custom_call" | custom-call | flops 28387049472 | bytes 40000000 | tf_op jit(solution)/shard_map/spread/pallas_call | solution.py:417
  115.9 15.0 %split.1 = (bf16[1504,4096]{1,0:T(8,128)(2,1)}, f32[1504,1024]{1,0:T(8,128)}) custom-call(s32[1]{0:T(128)} %bitcast.1.source, f32[1504,1024]{1,0:T(8,128)} %get-tuple-element.32.a, f32[1504,1024]{1,0:T(8,128)} %get-tuple-element.33.b, f32[1504,1024]{1,0:T(8,128)} %ours.1, f32[1504,1024]{1,0:T(8,128)} %theirs.1, f32[1504,1024]{1,0:T(8,128)} %get-tuple-element.34.q), custom_call_target="tpu_custom_call" | custom-call | flops 100000000 | bytes 25000000 | tf_op jit(solution)/shard_map/split/pallas_call | solution.py:453
  130.8 39.9 %update.4.refs_0_ = f32[1504,3008]{1,0:T(8,128)} custom-call(s32[4]{0:T(128)} %pad_add_fusion.1.tiles, bf16[1504,4096]{1,0:T(8,128)(2,1)} %get-tuple-element.35.slab, f32[1504,1024]{1,0:T(8,128)} %get-tuple-element.38.g, f32[1504,1024]{1,0:T(8,128)} %get-tuple-element.34.q, f32[1504,3008]{1,0:T(8,128)} %trailing.7), custom_call_target="tpu_custom_call" | custom-call | flops 28387049472 | bytes 27721728 | tf_op jit(solution)/shard_map/update/pallas_call | solution.py:526
  170.8 1.6 collective-permute-start.1
  172.8 1.6 collective-permute-start.5
  174.8 24.2 %collective-permute-done.4.panel = f32[1056,1024]{1,0:T(8,128)} collective-permute-done((f32[1056,1024]{1,0:T(8,128)}, f32[1056,1024]{1,0:T(8,128)}, u32[]{:S(2)}, u32[]{:S(2)}) %collective-permute-start.4) | collective-permute-done | bytes 4325408 | tf_op jit(solution)/shard_map/ppermute | solution.py:549
  199.1 25.7 %columns.1 = (f32[1056,1024]{1,0:T(8,128)}, f32[1056,1024]{1,0:T(8,128)}) custom-call(f32[1056,1024]{1,0:T(8,128)} %collective-permute-done.3.factor, f32[1056,1024]{1,0:T(8,128)} %collective-permute-done.4.panel, bf16[1024,1024]{1,0:T(8,128)(2,1)} %get-tuple-element.41.ih, bf16[1024,1024]{1,0:T(8,128)(2,1)} %get-tuple-element.42.il, ...), custom_call_target="tpu_custom_call" | custom-call | flops 19931332608 | bytes 17301504 | tf_op jit(solution)/shard_map/columns/pallas_call | solution.py:477
  224.7 1.7 fusion.3
  226.4 1.0 fusion.4
  227.4 28.6 %update.5.refs_0_ = f32[1504,3008]{1,0:T(8,128)} custom-call(s32[3]{0:T(128)} %pad_add_fusion.tiles, bf16[1504,4096]{1,0:T(8,128)(2,1)} %get-tuple-element.35.slab, f32[1056,1024]{1,0:T(8,128)} %get-tuple-element.45.g, f32[1056,1024]{1,0:T(8,128)} %get-tuple-element.46.q, f32[1504,3008]{1,0:T(8,128)} %trailing.7, ...), custom_call_target="tpu_custom_call", output_to_operand_aliasing={{}: (5, {})} | custom-call | flops 18924699648 | bytes 18481152 | tf_op jit(solution)/shard_map/update/pallas_call | solution.py:526
  256.1 1.6 copy-done.5
  258.3 1.5 pad_maximum_fusion.1.q
  259.9 0.7 slice-done
  260.9 1.4 pad_maximum_fusion.g
  262.3 18.2 %update.6.refs_0_ = f32[1504,3008]{1,0:T(8,128)} custom-call(s32[2]{0:T(128)} %pad_add_fusion.2.tiles, bf16[1504,4096]{1,0:T(8,128)(2,1)} %get-tuple-element.35.slab, f32[512,1024]{1,0:T(8,128)} %pad_maximum_fusion.g, f32[512,1024]{1,0:T(8,128)} %pad_maximum_fusion.1.q, f32[1504,3008]{1,0:T(8,128)} %trailing.7, ...), custom_call_target="tpu_custom_call", output_to_operand_aliasing={{}: (5, {})} | custom-call | flops 9462349824 | bytes 9240576 | tf_op jit(solution)/shard_map/update/pallas_call | solution.py:526
  280.6 3.3 %maximum_select_fusion.2 = (f32[256,1024]{1,0:T(8,128)}, f32[256,1024]{1,0:T(8,128)}) fusion(f32[32,1024]{1,0:T(8,128)S(1)} %copy-done.8, f32[192,1024]{1,0:T(8,128)S(1)} %collective-permute-done.5, f32[32,1024]{1,0:T(8,128)S(1)} %slice-done.2, f32[64,1024]{1,0:T(8,128)S(1)} %slice-done.1, pred[]{:T(512)S(6)} %eq.7, f32[64,1024]{1,0:T(8,128)S(1)} %slice-done.3, ...), kind=kLoop, calls=%fused_computation.6 | loop fusion | flops 2097152 | bytes 4718593 | tf_op jit(solution)/shard_map/jit(_where)/select_n | solution.py:593
  283.9 10.2 %update.7 = f32[1504,3008]{1,0:T(8,128)} custom-call(s32[1]{0:T(128)} %bitcast.tiles, bf16[1504,4096]{1,0:T(8,128)(2,1)} %get-tuple-element.35.slab, f32[256,1024]{1,0:T(8,128)} %get-tuple-element.71.g, f32[256,1024]{1,0:T(8,128)} %get-tuple-element.72.q, f32[1504,3008]{1,0:T(8,128)} %trailing.7, ...), custom_call_target="tpu_custom_call", output_to_operand_aliasing={{}: (5, {})} | custom-call | flops 4731174912 | bytes 4620288 | tf_op jit(solution)/shard_map/update/pallas_call | solution.py:526
  (50 shorter events, 4.1 us)
Async XLA Ops:
  1.9 8.0 %copy-start = (f32[1504,1024]{1,0:T(8,128)S(1)}, f32[1504,1024]{1,0:T(8,128)}, u32[]{:S(2)}) copy-start(f32[1504,1024]{1,0:T(8,128)} %ours.1) | copy-start | bytes 18481156
  1.9 14.2 %collective-permute-start = (f32[32,1152]{1,0:T(8,128)S(1)}, f32[32,1152]{1,0:T(8,128)S(1)}, u32[]{:S(2)}, u32[]{:S(2)}) collective-permute-start(f32[32,1152]{1,0:T(8,128)S(1)} %pad_maximum_fusion.4), channel_id=1, source_target_pairs={{0,1},{1,0},{2,3},{3,2},{4,5},{5,4},{6,7},{7,6},{8,9},{9,8},{10,11... | collective-permute-start | bytes 442376 | tf_op jit(solution)/shard_map/ppermute | solution.py:549
  9.8 164.6 %collective-permute-start.3 = (f32[1056,1024]{1,0:T(8,128)}, f32[1056,1024]{1,0:T(8,128)}, u32[]{:S(2)}, u32[]{:S(2)}) collective-permute-start(f32[1056,1024]{1,0:T(8,128)} %slice.36), channel_id=1, source_target_pairs={{0,1},{1,0},{2,3},{3,2},{4,5},{5,4},{6,7},{7,6},{8,9},{9,8},{10,11... | collective-permute-start | bytes 12976136 | tf_op jit(solution)/shard_map/ppermute | solution.py:549
  12.4 186.7 %collective-permute-start.4 = (f32[1056,1024]{1,0:T(8,128)}, f32[1056,1024]{1,0:T(8,128)}, u32[]{:S(2)}, u32[]{:S(2)}) collective-permute-start(f32[1056,1024]{1,0:T(8,128)} %slice.37), channel_id=1, source_target_pairs={{0,1},{1,0},{2,3},{3,2},{4,5},{5,4},{6,7},{7,6},{8,9},{9,8},{10,11... | collective-permute-start | bytes 12976136 | tf_op jit(solution)/shard_map/ppermute | solution.py:549
  170.8 85.2 %collective-permute-start.1 = (f32[256,1024]{1,0:T(8,128)}, f32[256,1024]{1,0:T(8,128)S(1)}, u32[]{:S(2)}, u32[]{:S(2)}) collective-permute-start(f32[256,1024]{1,0:T(8,128)} %get-tuple-element.36), channel_id=1, source_target_pairs={{0,1},{1,0},{2,3},{3,2},{4,5},{5,4},{6,7},{7,6},{8,9},{9,8},{10,11... | collective-permute-start | bytes 3145736 | tf_op jit(solution)/shard_map/ppermute | solution.py:549
  172.3 83.7 %collective-permute-start.2 = (f32[256,1024]{1,0:T(8,128)}, f32[256,1024]{1,0:T(8,128)S(1)}, u32[]{:S(2)}, u32[]{:S(2)}) collective-permute-start(f32[256,1024]{1,0:T(8,128)} %get-tuple-element.37), channel_id=1, source_target_pairs={{0,1},{1,0},{2,3},{3,2},{4,5},{5,4},{6,7},{7,6},{8,9},{9,8},{10,11... | collective-permute-start | bytes 3145736 | tf_op jit(solution)/shard_map/ppermute | solution.py:549
  172.8 107.7 %collective-permute-start.5 = (f32[192,1024]{1,0:T(8,128)}, f32[192,1024]{1,0:T(8,128)S(1)}, u32[]{:S(2)}, u32[]{:S(2)}) collective-permute-start(f32[192,1024]{1,0:T(8,128)} %get-tuple-element.50), channel_id=1, source_target_pairs={{0,1},{1,0},{2,3},{3,2},{4,5},{5,4},{6,7},{7,6},{8,9},{9,8},{10,11... | collective-permute-start | bytes 2359304 | tf_op jit(solution)/shard_map/ppermute | solution.py:549
  174.4 106.2 %collective-permute-start.6 = (f32[192,1024]{1,0:T(8,128)}, f32[192,1024]{1,0:T(8,128)}, u32[]{:S(2)}, u32[]{:S(2)}) collective-permute-start(f32[192,1024]{1,0:T(8,128)} %get-tuple-element.51), channel_id=1, source_target_pairs={{0,1},{1,0},{2,3},{3,2},{4,5},{5,4},{6,7},{7,6},{8,9},{9,8},{10,11... | collective-permute-start | bytes 2359304 | tf_op jit(solution)/shard_map/ppermute | solution.py:549
  256.0 1.8 copy-start.5
  256.0 1.9 copy-start.6
  256.0 2.0 copy-start.7
  256.0 2.2 copy-start.1
  256.0 2.2 copy-start.3
  258.0 1.8 copy-start.4
  258.3 1.6 copy-start.2
  258.3 2.3 slice-start
  262.3 18.2 %slice-start.1 = ((f32[256,1024]{1,0:T(8,128)}), f32[64,1024]{1,0:T(8,128)S(1)}, s32[]{:S(2)}) async-start(f32[256,1024]{1,0:T(8,128)} %copy-done.1), calls=%async_computation.1 | async-start | bytes 524288 | tf_op jit(solution)/shard_map/slice | solution.py:593
  262.3 18.2 %slice-start.2 = ((f32[256,1024]{1,0:T(8,128)}), f32[32,1024]{1,0:T(8,128)S(1)}, s32[]{:S(2)}) async-start(f32[256,1024]{1,0:T(8,128)} %copy-done.1), calls=%async_computation.2 | async-start | bytes 262144 | tf_op jit(solution)/shard_map/slice | solution.py:592
  262.3 18.2 %slice-start.3 = ((f32[256,1024]{1,0:T(8,128)}), f32[64,1024]{1,0:T(8,128)S(1)}, s32[]{:S(2)}) async-start(f32[256,1024]{1,0:T(8,128)} %copy-done.3), calls=%async_computation.3 | async-start | bytes 524288 | tf_op jit(solution)/shard_map/slice | solution.py:593
  262.3 18.2 %slice-start.4 = ((f32[256,1024]{1,0:T(8,128)}), f32[32,1024]{1,0:T(8,128)S(1)}, s32[]{:S(2)}) async-start(f32[256,1024]{1,0:T(8,128)} %copy-done.3), calls=%async_computation.4 | async-start | bytes 262144 | tf_op jit(solution)/shard_map/slice | solution.py:592
  262.3 18.2 %copy-start.8 = (f32[32,1024]{1,0:T(8,128)S(1)}, f32[32,1024]{1,0:T(8,128)}, u32[]{:S(2)}) copy-start(f32[32,1024]{1,0:T(8,128)} %get-tuple-element.56) | copy-start | bytes 393220
  262.3 18.2 %copy-start.9 = (f32[32,1024]{1,0:T(8,128)S(1)}, f32[32,1024]{1,0:T(8,128)}, u32[]{:S(2)}) copy-start(f32[32,1024]{1,0:T(8,128)} %get-tuple-element.58) | copy-start | bytes 393220
  283.9 10.2 %copy-start.10 = (f32[32,1024]{1,0:T(8,128)S(1)}, f32[32,1024]{1,0:T(8,128)}, u32[]{:S(2)}) copy-start(f32[32,1024]{1,0:T(8,128)} %get-tuple-element.78) | copy-start | bytes 393220
